TPU v7x, 32 devices: a whole 2x2x4 slice. The times are simulated.
32 devices in a mesh: dp: 8 (over y, x, core), tensor: 4 (over z).
Axes of the slice: x: 2, y: 2, z: 4, core: 2. Of those that a mesh axis runs over, the one named last changes fastest.
Arguments:
- block_input: float32 [16384, 768], P(('dp', 'tensor'))
- cotangent: float32 [16384, 768], P(('dp', 'tensor')), may hold values from -6 to 6
- segment_ids: int32 [16384], P('dp'), may hold values from 0 to 2047, as said below
- token_offset: int32 [16384], P('dp'), may hold values from 0 to 2047, as said below
- first_gain: float32 [768], P(('dp', 'tensor')), may hold values from 0.1 to 1.9
- first_shift: float32 [768], P(('dp', 'tensor')), may hold values from -3 to 3
- second_gain: float32 [768], P(('dp', 'tensor')), may hold values from 0.1 to 1.9
- second_shift: float32 [768], P(('dp', 'tensor')), may hold values from -3 to 3
- qkv_weight: bfloat16 [3, 768, 768], P(None, 'dp', 'tensor')
- qkv_bias: bfloat16 [3, 768], P(None, ('tensor', 'dp')), may hold values from -3 to 3
- proj_weight: bfloat16 [768, 768], P('tensor', 'dp'), may hold values from -0.875 to 0.875
- up_weight: bfloat16 [768, 3072], P('dp', 'tensor'), may hold values from -0.21875 to 0.21875
- up_bias: bfloat16 [3072], P(('tensor', 'dp')), may hold values from -3 to 3
- down_weight: bfloat16 [3072, 768], P('tensor', 'dp'), may hold values from -0.109375 to 0.109375
- out_bias: float32 [768], P(('dp', 'tensor')), may hold values from -3 to 3
Outputs:
- block_output: float32 [16384, 768], P(('dp', 'tensor'))
- input_grad: float32 [16384, 768], P(('dp', 'tensor'))
- first_gain_grad: float32 [768], P(('dp', 'tensor'))
- first_shift_grad: float32 [768], P(('dp', 'tensor'))
- second_gain_grad: float32 [768], P(('dp', 'tensor'))
- second_shift_grad: float32 [768], P(('dp', 'tensor'))
- qkv_weight_grad: float32 [3, 768, 768], P(None, 'dp', 'tensor')
- qkv_bias_grad: float32 [3, 768], P(None, ('tensor', 'dp'))
- proj_weight_grad: float32 [768, 768], P('tensor', 'dp')
- up_weight_grad: float32 [768, 3072], P('dp', 'tensor')
- up_bias_grad: float32 [3072], P(('tensor', 'dp'))
- down_weight_grad: float32 [3072, 768], P('tensor', 'dp')
- out_bias_grad: float32 [768], P(('dp', 'tensor'))
Inputs may be any that keep to these rules, and one draw needn't show every extreme that they name: `segment_ids`: within each block of 2048 tokens of one index of dp, segment numbers start at 0 and rise by one where a new sequence begins; in every draw some block holds one sequence and some other block gives every token a sequence of its own. `token_offset`: 0 at a sequence's first token, one more than the previous token's otherwise; in every draw some block of 2048 tokens holds one sequence.
All inputs are finite; a program needn't handle non-finite values.
Results may differ from a plain program's by a relative error of at most 0.009.
Values may be sent and summed in bfloat16 or wider, within the bound.
A program may use at most 192 MiB of HBM per device.

v0:
```python
import jax
import jax.numpy as jnp
from jax import lax
from jax.sharding import PartitionSpec as P

HD = 64
ROT = 16


EPSILON = 1e-05
NEGATIVE = -1e30


def gelu_exact(values):
    return 0.5 * values * (1.0 + jax.scipy.special.erf(values * 0.7071067811865476))


def gelu_slope(values):
    return (
        0.5 * (1.0 + jax.scipy.special.erf(values * 0.7071067811865476))
        + values * jnp.exp(-0.5 * values * values) * 0.3989422804014327
    )


def norm_rows(rows, gain, shift):
    center = rows - jnp.mean(rows, axis=1, keepdims=True)
    inverse = lax.rsqrt(jnp.mean(center * center, axis=1, keepdims=True) + EPSILON)
    normal = center * inverse
    return (normal, inverse, normal * gain + shift)


def norm_back(grad_out, normal, inverse, gain):
    scaled = grad_out * gain
    return inverse * (
        scaled
        - jnp.mean(scaled, axis=1, keepdims=True)
        - normal * jnp.mean(scaled * normal, axis=1, keepdims=True)
    )


def rotary_tables(offsets):
    half = ROT // 2
    freq = 10000.0 ** (-(2.0 * jnp.arange(half, dtype=jnp.float32)) / ROT)
    angles = offsets.astype(jnp.float32)[:, None] * freq[None, :]
    return (jnp.cos(angles)[:, None, :], jnp.sin(angles)[:, None, :])


def rotate(values, cosine, sine):
    half = ROT // 2
    first = values[..., :half]
    second = values[..., half:ROT]
    return jnp.concatenate(
        [first * cosine - second * sine, second * cosine + first * sine, values[..., ROT:]], axis=-1
    )


def masked_scores(block_query, keys, block_seg, key_seg, low, scale):
    scores = (
        jnp.einsum("qhd,khd->hqk", block_query, keys, preferred_element_type=jnp.float32) * scale
    )
    rows = low + jnp.arange(block_query.shape[0], dtype=jnp.int32)[:, None]
    cols = jnp.arange(keys.shape[0], dtype=jnp.int32)[None, :]
    allowed = (block_seg[:, None] == key_seg[None, :]) & (cols <= rows)
    return jnp.where(allowed[None], scores, NEGATIVE)


def shards(
    block_input,
    cotangent,
    segment_ids,
    token_offset,
    first_gain,
    first_shift,
    second_gain,
    second_shift,
    qkv_weight,
    qkv_bias,
    proj_weight,
    up_weight,
    up_bias,
    down_weight,
    out_bias,
):
    scale = HD ** (-0.5)
    width_model = block_input.shape[1]
    gain_one, shift_one, gain_two, shift_two, bias_out = (
        lax.all_gather(first_gain, ("dp", "tensor"), axis=0, tiled=True),
        lax.all_gather(first_shift, ("dp", "tensor"), axis=0, tiled=True),
        lax.all_gather(second_gain, ("dp", "tensor"), axis=0, tiled=True),
        lax.all_gather(second_shift, ("dp", "tensor"), axis=0, tiled=True),
        lax.all_gather(out_bias, ("dp", "tensor"), axis=0, tiled=True),
    )
    normal_one, inverse_one, mixed_one = norm_rows(block_input, gain_one, shift_one)
    normal_two, inverse_two, mixed_two = norm_rows(block_input, gain_two, shift_two)
    attn_rows, ffn_rows = (
        lax.all_gather(mixed_one.astype(jnp.bfloat16), "tensor", axis=0, tiled=True),
        lax.all_gather(mixed_two.astype(jnp.bfloat16), "tensor", axis=0, tiled=True),
    )
    full_qkv, full_qkv_bias, full_proj, full_up, full_up_bias, full_down = (
        lax.all_gather(qkv_weight, "dp", axis=1, tiled=True),
        lax.all_gather(qkv_bias, "dp", axis=1, tiled=True),
        lax.all_gather(proj_weight, "dp", axis=1, tiled=True),
        lax.all_gather(up_weight, "dp", axis=0, tiled=True),
        lax.all_gather(up_bias, "dp", axis=0, tiled=True),
        lax.all_gather(down_weight, "dp", axis=1, tiled=True),
    )
    total = attn_rows.shape[0]
    projected = (
        jnp.einsum("td,kde->kte", attn_rows, full_qkv, preferred_element_type=jnp.float32)
        + full_qkv_bias.astype(jnp.float32)[:, None, :]
    )
    local_width = projected.shape[2]
    heads = local_width // HD
    cosine, sine = rotary_tables(token_offset)
    query = rotate(projected[0].reshape(total, heads, HD), cosine, sine).astype(jnp.bfloat16)
    keys = rotate(projected[1].reshape(total, heads, HD), cosine, sine).astype(jnp.bfloat16)
    values = projected[2].reshape(total, heads, HD).astype(jnp.bfloat16)
    block_rows = min(512, total)
    block_count = total // block_rows
    out_parts = []
    log_parts = []
    for row_block in range(block_count):
        low = row_block * block_rows
        high = low + block_rows
        scores = masked_scores(
            query[low:high], keys[:high], segment_ids[low:high], segment_ids[:high], low, scale
        )
        peak = jnp.max(scores, axis=2, keepdims=True)
        weights = jnp.exp(scores - peak)
        mass = jnp.sum(weights, axis=2, keepdims=True)
        probs = (weights / mass).astype(jnp.bfloat16)
        out_parts.append(
            jnp.einsum("hqk,khd->qhd", probs, values[:high], preferred_element_type=jnp.float32)
        )
        log_parts.append(peak + jnp.log(mass))
    attended = jnp.concatenate(out_parts, axis=0).astype(jnp.bfloat16)
    logsum = jnp.concatenate(log_parts, axis=1)
    attended_flat = attended.reshape(total, local_width)
    hidden_pre = jnp.dot(
        ffn_rows, full_up, preferred_element_type=jnp.float32
    ) + full_up_bias.astype(jnp.float32)
    activ = gelu_exact(hidden_pre).astype(jnp.bfloat16)
    branch_sum = lax.psum_scatter(
        jnp.dot(attended_flat, full_proj, preferred_element_type=jnp.float32)
        + jnp.dot(activ, full_down, preferred_element_type=jnp.float32),
        "tensor",
        scatter_dimension=0,
        tiled=True,
    )
    block_output = block_input + branch_sum + bias_out
    out_bias_part = jnp.sum(cotangent, axis=0)
    grad_rows = lax.all_gather(cotangent.astype(jnp.bfloat16), "tensor", axis=0, tiled=True)
    back_qkv, back_proj, back_up, back_down = (
        lax.all_gather(qkv_weight, "dp", axis=1, tiled=True),
        lax.all_gather(proj_weight, "dp", axis=1, tiled=True),
        lax.all_gather(up_weight, "dp", axis=0, tiled=True),
        lax.all_gather(down_weight, "dp", axis=1, tiled=True),
    )
    proj_grad = jnp.einsum(
        "te,td->ed", attended_flat, grad_rows, preferred_element_type=jnp.float32
    )
    down_grad = jnp.einsum("tf,td->fd", activ, grad_rows, preferred_element_type=jnp.float32)
    attended_grad = (
        jnp.einsum("td,ed->te", grad_rows, back_proj, preferred_element_type=jnp.float32)
        .astype(jnp.bfloat16)
        .reshape(total, heads, HD)
    )
    pre_grad = jnp.einsum(
        "td,fd->tf", grad_rows, back_down, preferred_element_type=jnp.float32
    ) * gelu_slope(hidden_pre)
    up_bias_part = jnp.sum(pre_grad, axis=0)
    pre_round = pre_grad.astype(jnp.bfloat16)
    up_grad = jnp.einsum("td,tf->df", ffn_rows, pre_round, preferred_element_type=jnp.float32)
    delta = jnp.einsum("thd,thd->ht", attended_grad, attended, preferred_element_type=jnp.float32)
    key_grad = jnp.zeros((total, heads, HD), jnp.float32)
    value_grad = jnp.zeros((total, heads, HD), jnp.float32)
    query_parts = []
    for row_block in range(block_count):
        low = row_block * block_rows
        high = low + block_rows
        scores = masked_scores(
            query[low:high], keys[:high], segment_ids[low:high], segment_ids[:high], low, scale
        )
        probs = jnp.exp(scores - logsum[:, low:high])
        block_grad = attended_grad[low:high]
        value_grad = value_grad.at[:high].add(
            jnp.einsum(
                "hqk,qhd->khd",
                probs.astype(jnp.bfloat16),
                block_grad,
                preferred_element_type=jnp.float32,
            )
        )
        prob_grad = jnp.einsum(
            "qhd,khd->hqk", block_grad, values[:high], preferred_element_type=jnp.float32
        )
        score_round = (probs * (prob_grad - delta[:, low:high, None]) * scale).astype(jnp.bfloat16)
        query_parts.append(
            jnp.einsum("hqk,khd->qhd", score_round, keys[:high], preferred_element_type=jnp.float32)
        )
        key_grad = key_grad.at[:high].add(
            jnp.einsum(
                "hqk,qhd->khd", score_round, query[low:high], preferred_element_type=jnp.float32
            )
        )
    query_grad = rotate(jnp.concatenate(query_parts, axis=0), cosine, -sine)
    key_grad = rotate(key_grad, cosine, -sine)
    stacked = jnp.stack([query_grad, key_grad, value_grad]).reshape(3, total, local_width)
    qkv_bias_part = jnp.sum(stacked, axis=1)
    stacked_round = stacked.astype(jnp.bfloat16)
    qkv_grad = jnp.einsum(
        "td,kte->kde", attn_rows, stacked_round, preferred_element_type=jnp.float32
    )
    first = jnp.einsum("kte,kde->td", stacked_round, back_qkv, preferred_element_type=jnp.float32)
    second = jnp.einsum("tf,df->td", pre_round, back_up, preferred_element_type=jnp.float32)
    both = lax.psum_scatter(
        jnp.concatenate([first, second], axis=1), "tensor", scatter_dimension=0, tiled=True
    )
    grad_one = both[:, :width_model]
    grad_two = both[:, width_model:]
    input_grad = (
        cotangent
        + norm_back(grad_one, normal_one, inverse_one, gain_one)
        + norm_back(grad_two, normal_two, inverse_two, gain_two)
    )
    gain_one_grad, shift_one_grad, gain_two_grad, shift_two_grad, bias_out_grad = (
        lax.psum_scatter(
            jnp.sum(grad_one * normal_one, axis=0),
            ("dp", "tensor"),
            scatter_dimension=0,
            tiled=True,
        ),
        lax.psum_scatter(
            jnp.sum(grad_one, axis=0), ("dp", "tensor"), scatter_dimension=0, tiled=True
        ),
        lax.psum_scatter(
            jnp.sum(grad_two * normal_two, axis=0),
            ("dp", "tensor"),
            scatter_dimension=0,
            tiled=True,
        ),
        lax.psum_scatter(
            jnp.sum(grad_two, axis=0), ("dp", "tensor"), scatter_dimension=0, tiled=True
        ),
        lax.psum_scatter(out_bias_part, ("dp", "tensor"), scatter_dimension=0, tiled=True),
    )
    (
        qkv_weight_grad,
        qkv_bias_grad,
        proj_weight_grad,
        up_weight_grad,
        up_bias_grad,
        down_weight_grad,
    ) = (
        lax.psum_scatter(qkv_grad, "dp", scatter_dimension=1, tiled=True),
        lax.psum_scatter(qkv_bias_part, "dp", scatter_dimension=1, tiled=True),
        lax.psum_scatter(proj_grad, "dp", scatter_dimension=1, tiled=True),
        lax.psum_scatter(up_grad, "dp", scatter_dimension=0, tiled=True),
        lax.psum_scatter(up_bias_part, "dp", scatter_dimension=0, tiled=True),
        lax.psum_scatter(down_grad, "dp", scatter_dimension=1, tiled=True),
    )
    return (
        block_output,
        input_grad,
        gain_one_grad,
        shift_one_grad,
        gain_two_grad,
        shift_two_grad,
        qkv_weight_grad,
        qkv_bias_grad,
        proj_weight_grad,
        up_weight_grad,
        up_bias_grad,
        down_weight_grad,
        bias_out_grad,
    )


def solution(mesh):
    return jax.shard_map(
        shards,
        mesh=mesh,
        in_specs=(
            P(("dp", "tensor"), None),
            P(("dp", "tensor"), None),
            P("dp"),
            P("dp"),
            P(("dp", "tensor")),
            P(("dp", "tensor")),
            P(("dp", "tensor")),
            P(("dp", "tensor")),
            P(None, "dp", "tensor"),
            P(None, ("tensor", "dp")),
            P("tensor", "dp"),
            P("dp", "tensor"),
            P(("tensor", "dp")),
            P("tensor", "dp"),
            P(("dp", "tensor")),
        ),
        out_specs=(
            P(("dp", "tensor"), None),
            P(("dp", "tensor"), None),
            P(("dp", "tensor")),
            P(("dp", "tensor")),
            P(("dp", "tensor")),
            P(("dp", "tensor")),
            P(None, "dp", "tensor"),
            P(None, ("tensor", "dp")),
            P("tensor", "dp"),
            P("dp", "tensor"),
            P(("tensor", "dp")),
            P("tensor", "dp"),
            P(("dp", "tensor")),
        ),
        check_vma=False,
    )
```

profile of v0, /device:TPU:0, one launch (start us, length us, event | category | flops | bytes accessed | tf_op | source)
XLA Modules:
  0.0 807.5 jit_solution(4287615499470747536)
XLA Ops:
  11.8 42.2 %all-reduce.16 = (f32[768]{0:T(1024)S(1)}, f32[768]{0:T(1024)S(1)}, f32[768]{0:T(1024)S(1)}, f32[768]{0:T(1024)S(1)}) all-reduce(f32[768]{0:T(1024)S(1)} %dynamic-update-slice.25, f32[768]{0:T(1024)S(1)} %dynamic-update-slice.24, f32[768]{0:T(1024)S(1)} %dynamic-update-slice.23, ...), channel_id=1, replica_groups=mesh['dp'=8,'tensor'=4] {'dp','tensor'}, use_global_device_ids=true, to_apply=%add.5 | all-reduce | flops 3072 | bytes 24576
  59.5 12.9 %all_gather.49 = bf16[3,768,192]{2,0,1:T(4,128)(2,1)S(1)} all-gather(bf16[3,96,192]{2,0,1:T(4,128)(2,1)S(1)} %copy.62), channel_id=1, replica_groups=mesh['dp'=8,'tensor'=4] {'dp'}, dimensions={1}, use_global_device_ids=true | all-gather | bytes 995328 | tf_op jit(solution)/shard_map/all_gather | solution.py:100
  73.3 9.1 %all-gather = bf16[8,24,3]{1,2,0:T(4,128)(2,1)S(1)} all-gather(bf16[1,24,3]{1,2,0:T(4,128)(2,1)S(1)} %bitcast.207), channel_id=1, replica_groups=mesh['dp'=8,'tensor'=4] {'dp'}, dimensions={0}, use_global_device_ids=true | all-gather | bytes 1296 | tf_op jit(solution)/shard_map/all_gather | solution.py:101
  83.5 8.4 %all_gather.51 = bf16[192,768]{0,1:T(8,128)(2,1)S(1)} all-gather(bf16[192,96]{0,1:T(8,128)(2,1)S(1)} %copy.66), channel_id=1, replica_groups=mesh['dp'=8,'tensor'=4] {'dp'}, dimensions={1}, use_global_device_ids=true | all-gather | bytes 331776 | tf_op jit(solution)/shard_map/all_gather | solution.py:102
  93.5 14.2 %all-reduce.6 = bf16[768]{0:T(1024)(128)(2,1)S(1)} all-reduce(bf16[768]{0:T(1024)(128)(2,1)S(1)} %dynamic-update-slice.26), channel_id=1, replica_groups=mesh['dp'=8,'tensor'=4] {'dp'}, use_global_device_ids=true, to_apply=%add.6 | all-reduce | flops 768 | bytes 3072
  109.2 2.2 fusion.20
  114.5 4.6 all-gather.7.cloned.1.call-done
  119.1 3.9 fusion.123
  131.9 2.9 fusion.83
  138.3 2.2 copy-done
  140.4 2.9 fusion.81
  143.4 5.9 fusion.4
  149.3 6.8 fusion
  156.8 7.4 fusion.84
  164.1 18.7 %all-gather.15.cloned.1.call-done = bf16[2048,768]{1,0:T(8,128)(2,1)} async-done(((bf16[512,768]{1,0:T(8,128)(2,1)}), bf16[2048,768]{1,0:T(8,128)(2,1)}) %all-gather.15.cloned.1.call-update) | async-done | bytes 3145744 | tf_op jit(solution)/shard_map/all_gather | solution.py:152
  182.8 3.2 convolution_convert_fusion
  190.0 3.2 multiply_convert_fusion.2
  195.1 2.7 multiply_convert_fusion.1
  197.9 2.3 convolution_bitcast_fusion.9
  200.2 8.1 %multiply_convert_fusion = bf16[3,512,2048]{2,1,0:T(8,128)(2,1)S(1)} fusion(f32[3,512,2048]{2,1,0:T(8,128)} %get-tuple-element.249, f32[3,512]{1,0:T(4,128)S(1)} %get-tuple-element.229, f32[3,512]{1,0:T(4,128)S(1)} %copy-done.79, pred[512,2048]{1,0:T(8,128)(4,1)S(1)} %copy-done.13, bf16[512,3,64]{0,2,1:T(8,128)(2,1)S(1)} %bitcast.200, ...), kind=kOutput, calls=%fused_computation.1 | convolution fusion | flops 424673280 | bytes 20918272 | tf_op jit(solution)/shard_map/qhd,khd->hqk/dot_general | solution.py:194
  214.3 2.2 convolution_bitcast_fusion.3
  216.5 5.1 fusion.73
  221.7 5.5 fusion.45
  227.2 7.8 fusion.48
  241.1 3.2 fusion.62
  244.3 3.0 copy.90
  247.3 2.8 reshape.664
  250.3 21.9 %all-gather.9.cloned.1.call-done = bf16[2048,768]{1,0:T(8,128)(2,1)} async-done(((bf16[512,768]{1,0:T(8,128)(2,1)}), bf16[2048,768]{1,0:T(8,128)(2,1)}) %all-gather.9.cloned.1.call-update) | async-done | bytes 3145744 | tf_op jit(solution)/shard_map/all_gather | solution.py:97
  272.2 7.2 multiply_convert_fusion.3
  279.4 4.6 convolution_bitcast_fusion
  284.0 12.5 %all-gather.13.cloned.1.call-done = bf16[768,768]{0,1:T(8,128)(2,1)} async-done(((bf16[768,96]{0,1:T(8,128)(2,1)}), bf16[768,768]{0,1:T(8,128)(2,1)}) %all-gather.13.cloned.1.call-update) | async-done | bytes 1179664 | tf_op jit(solution)/shard_map/all_gather | solution.py:105
  296.5 7.0 fusion.122
  305.2 4.5 fusion.58
  309.8 10.9 %pad_maximum_fusion = f32[2048,1536]{1,0:T(8,128)} fusion(f32[2048,768]{1,0:T(8,128)} %fusion.58, f32[2048,768]{1,0:T(8,128)} %convolution_bitcast_fusion), kind=kLoop, calls=%fused_computation | loop fusion | flops 3145728 | bytes 25165824 | tf_op jit(solution)/shard_map/concatenate | solution.py:217
  321.9 4.6 fusion.124
  326.6 3.6 convolution_add_fusion
  330.3 6.9 fusion.56
  337.4 6.9 fusion.125
  346.0 2.3 fusion.21
  348.4 13.6 %all-reduce.17 = (f32[3,192]{1,0:T(4,128)S(1)}, f32[768]{0:T(1024)S(1)}) all-reduce(f32[3,192]{1,0:T(4,128)S(1)} %fusion.21, f32[768]{0:T(1024)S(1)} %get-tuple-element.252), channel_id=9, replica_groups=mesh['dp'=8,'tensor'=4] {'dp'}, use_global_device_ids=true, to_apply=%region_26.27.clone | all-reduce | flops 1344 | bytes 10752
  365.0 13.2 %reduce-scatter.20.cloned.1.call-done = f32[96,576]{1,0:T(8,128)} async-done(((f32[768,576]{1,0:T(8,128)}), f32[96,576]{1,0:T(8,128)}) %reduce-scatter.20.cloned.1.call-update) | async-done | bytes 221200
  380.0 212.4 %reduce-scatter.14.cloned.1.call-done = f32[512,1536]{1,0:T(8,128)} async-done(((f32[2048,1536]{1,0:T(8,128)}), f32[512,1536]{1,0:T(8,128)}) %reduce-scatter.14.cloned.1.call-update) | async-done | bytes 3145744 | tf_op jit(solution)/shard_map/reduce_scatter | solution.py:216
  592.4 3.1 slice_reduce_fusion
  595.5 50.1 %all-reduce.15 = (f32[768]{0:T(1024)S(1)}, f32[768]{0:T(1024)S(1)}, f32[768]{0:T(1024)S(1)}, f32[768]{0:T(1024)S(1)}, f32[768]{0:T(1024)S(1)}, /*index=5*/f32[768]{0:T(1024)S(1)}) all-reduce(f32[768]{0:T(1024)S(1)} %copy-done.76, f32[768]{0:T(1024)S(1)} %get-tuple-element.187, ...), channel_id=1, replica_groups=mesh['dp'=8,'tensor'=4] {'dp','tensor'}, use_global_device_ids=true, to_apply=%add.7 | all-reduce | flops 4608 | bytes 36864
  648.6 59.1 %reduce-scatter.12.cloned.1.call-done = f32[512,768]{1,0:T(8,128)} async-done(((f32[2048,768]{1,0:T(8,128)}), f32[512,768]{1,0:T(8,128)}) %reduce-scatter.12.cloned.1.call-update) | async-done | bytes 1572880 | tf_op jit(solution)/shard_map/reduce_scatter | solution.py:143
  707.6 3.9 multiply_add_fusion
  711.5 42.7 %reduce-scatter.16.cloned.1.call-done = f32[96,768]{1,0:T(8,128)} async-done(((f32[768,768]{1,0:T(8,128)}), f32[96,768]{1,0:T(8,128)}) %reduce-scatter.16.cloned.1.call-update) | async-done | bytes 294928 | tf_op jit(solution)/shard_map/reduce_scatter | solution.py:258
  754.3 46.3 %reduce-scatter.18.cloned.1.call-done = f32[768,96]{0,1:T(8,128)} async-done(((f32[768,768]{0,1:T(8,128)}), f32[768,96]{0,1:T(8,128)}) %reduce-scatter.18.cloned.1.call-update) | async-done | bytes 294928 | tf_op jit(solution)/shard_map/reduce_scatter | solution.py:260
  (316 shorter events, 58.9 us)
Async XLA Ops:
  7.2 46.8 %copy-start.1 = (f32[512,768]{1,0:T(8,128)S(1)}, f32[512,768]{1,0:T(8,128)}, u32[]{:S(2)}) copy-start(f32[512,768]{1,0:T(8,128)} %param.35) | copy-start | bytes 4718596
  7.2 111.9 %all-gather.7.cloned.1.call-start = ((), (), s32[]{:S(2)}) async-start(), calls=%async_computation.6 | async-start | bytes 3932160 | tf_op jit(solution)/shard_map/all_gather | solution.py:96
  8.9 46.8 %copy-start.5 = (f32[512,768]{1,0:T(8,128)S(1)}, f32[512,768]{1,0:T(8,128)}, u32[]{:S(2)}) copy-start(f32[512,768]{1,0:T(8,128)} %param.36) | copy-start | bytes 4718596
  9.0 48.3 %copy-start.66 = (f32[512]{0:T(512)}, f32[512]{0:T(512)S(1)}, u32[]{:S(2)}) copy-start(f32[512]{0:T(512)S(1)} %broadcast_multiply_fusion.4) | copy-start | bytes 6148
  10.8 46.5 %copy-start.73 = (f32[512]{0:T(512)}, f32[512]{0:T(512)S(1)}, u32[]{:S(2)}) copy-start(f32[512]{0:T(512)S(1)} %add_rsqrt_fusion) | copy-start | bytes 6148
  55.7 127.1 %all-gather.15.cloned.1.call-start = ((), (), s32[]{:S(2)}) async-start(), calls=%async_computation.11 | async-start | bytes 3932160 | tf_op jit(solution)/shard_map/all_gather | solution.py:152
  57.3 16.0 %copy-start.84 = (bf16[3,24]{1,0:T(4,128)(2,1)S(1)}, bf16[3,24]{1,0:T(4,128)(2,1)}, u32[]{:S(2)}) copy-start(bf16[3,24]{1,0:T(4,128)(2,1)} %param.44) | copy-start | bytes 436
  57.3 25.1 %copy-start.81 = (s32[2048]{0:T(1024)S(1)}, s32[2048]{0:T(1024)}, u32[]{:S(2)}) copy-start(s32[2048]{0:T(1024)} %param.38) | copy-start | bytes 24580
  57.4 26.0 %copy-start.68 = (bf16[192,96]{1,0:T(8,128)(2,1)S(1)}, bf16[192,96]{1,0:T(8,128)(2,1)}, u32[]{:S(2)}) copy-start(bf16[192,96]{1,0:T(8,128)(2,1)} %param.45) | copy-start | bytes 110596
  57.4 192.9 %all-gather.11.cloned.1.call-start = ((), (), s32[]{:S(2)}) async-start(), calls=%async_computation.8 | async-start | bytes 1327104 | tf_op jit(solution)/shard_map/all_gather | solution.py:103
  58.1 214.1 %all-gather.9.cloned.1.call-start = ((), (), s32[]{:S(2)}) async-start(), calls=%async_computation.7 | async-start | bytes 3932160 | tf_op jit(solution)/shard_map/all_gather | solution.py:97
  58.2 33.8 %copy-start.83 = (u32[32]{0:T(128)S(1)}, u32[32]{0:T(128)}, u32[]{:S(2)}) copy-start(u32[32]{0:T(128)} %constant.270) | copy-start | bytes 388
  58.2 35.1 %copy-start.92 = (bf16[96]{0:T(256)(128)(2,1)S(1)}, bf16[96]{0:T(256)(128)(2,1)}, u32[]{:S(2)}) copy-start(bf16[96]{0:T(256)(128)(2,1)} %param.47) | copy-start | bytes 580
  58.7 237.8 %all-gather.13.cloned.1.call-start = ((), (), s32[]{:S(2)}) async-start(), calls=%async_computation.9 | async-start | bytes 1327104 | tf_op jit(solution)/shard_map/all_gather | solution.py:105
  59.3 303.9 %reduce-scatter.22.cloned.1.call-start = ((), (), s32[]{:S(2)}) async-start(), calls=%async_computation.16 | async-start | bytes 884736
  59.5 51.9 %slice-start.5 = ((s32[2048]{0:T(1024)}), s32[1024]{0:T(1024)S(1)}, s32[]{:S(2)}) async-start(s32[2048]{0:T(1024)} %param.37), calls=%async_computation.22 | async-start | bytes 8192 | tf_op jit(solution)/shard_map/slice | solution.py:126
  73.3 49.8 %copy-start.38 = (bf16[3,768,192]{1,2,0:T(8,128)(2,1)}, bf16[3,768,192]{1,2,0:T(8,128)(2,1)S(1)}, u32[]{:S(2)}) copy-start(bf16[3,768,192]{1,2,0:T(8,128)(2,1)S(1)} %copy.63) | copy-start | bytes 2654212
  91.9 90.9 %copy-start.20 = (bf16[192,768]{0,1:T(8,128)(2,1)}, bf16[192,768]{0,1:T(8,128)(2,1)S(1)}, u32[]{:S(2)}) copy-start(bf16[192,768]{0,1:T(8,128)(2,1)S(1)} %all_gather.51) | copy-start | bytes 884740
  109.2 14.9 %copy-start.37 = (f32[2048,8]{0,1:T(8,128)}, f32[2048,8]{0,1:T(8,128)S(1)}, u32[]{:S(2)}) copy-start(f32[2048,8]{0,1:T(8,128)S(1)} %get-tuple-element.235) | copy-start | bytes 196612
  123.6 8.2 %copy-start.58 = (bf16[1,1024,192]{1,2,0:T(8,128)(2,1)}, bf16[1,1024,192]{1,2,0:T(8,128)(2,1)S(1)}, u32[]{:S(2)}) copy-start(bf16[1,1024,192]{1,2,0:T(8,128)(2,1)S(1)} %slice.413) | copy-start | bytes 1179652
  123.7 14.6 %copy-start.25 = (bf16[1,1536,192]{1,2,0:T(8,128)(2,1)}, bf16[1,1536,192]{1,2,0:T(8,128)(2,1)S(1)}, u32[]{:S(2)}) copy-start(bf16[1,1536,192]{1,2,0:T(8,128)(2,1)S(1)} %slice.416) | copy-start | bytes 1769476
  123.8 33.0 %copy-start.42 = (bf16[1,2048,192]{1,2,0:T(8,128)(2,1)}, bf16[1,2048,192]{1,2,0:T(8,128)(2,1)S(1)}, u32[]{:S(2)}) copy-start(bf16[1,2048,192]{1,2,0:T(8,128)(2,1)S(1)} %slice.419) | copy-start | bytes 2359300
  124.1 19.3 %copy-start.3 = (bf16[2048,3,48]{0,2,1:T(8,128)(2,1)}, bf16[2048,3,48]{0,2,1:T(8,128)(2,1)S(1)}, u32[]{:S(2)}) copy-start(bf16[2048,3,48]{0,2,1:T(8,128)(2,1)S(1)} %slice.496) | copy-start | bytes 1769476
  124.3 19.1 %copy-start.31 = (bf16[2048,3,8]{0,2,1:T(8,128)(2,1)}, bf16[2048,3,8]{0,2,1:T(8,128)(2,1)S(1)}, u32[]{:S(2)}) copy-start(bf16[2048,3,8]{0,2,1:T(8,128)(2,1)S(1)} %get-tuple-element.212) | copy-start | bytes 294916
  124.3 19.1 %copy-start.33 = (bf16[2048,3,8]{0,2,1:T(8,128)(2,1)}, bf16[2048,3,8]{0,2,1:T(8,128)(2,1)S(1)}, u32[]{:S(2)}) copy-start(bf16[2048,3,8]{0,2,1:T(8,128)(2,1)S(1)} %get-tuple-element.213) | copy-start | bytes 294916
  124.5 10.3 %copy-start.15 = (bf16[2048,3,64]{0,2,1:T(8,128)(2,1)}, bf16[2048,3,64]{0,2,1:T(8,128)(2,1)S(1)}, u32[]{:S(2)}) copy-start(bf16[2048,3,64]{0,2,1:T(8,128)(2,1)S(1)} %get-tuple-element.255) | copy-start | bytes 2359300
  124.5 18.9 %copy-start.22 = (bf16[2048,3,64]{0,2,1:T(8,128)(2,1)}, bf16[2048,3,64]{0,2,1:T(8,128)(2,1)S(1)}, u32[]{:S(2)}) copy-start(bf16[2048,3,64]{0,2,1:T(8,128)(2,1)S(1)} %get-tuple-element.254) | copy-start | bytes 2359300
  186.1 9.0 %copy-start.29 = (bf16[512,192]{0,1:T(8,128)(2,1)}, bf16[512,192]{0,1:T(8,128)(2,1)S(1)}, u32[]{:S(2)}) copy-start(bf16[512,192]{0,1:T(8,128)(2,1)S(1)} %get-tuple-element.223) | copy-start | bytes 589828
  186.1 14.1 %copy-start.61 = (bf16[512,192]{0,1:T(8,128)(2,1)}, bf16[512,192]{0,1:T(8,128)(2,1)S(1)}, u32[]{:S(2)}) copy-start(bf16[512,192]{0,1:T(8,128)(2,1)S(1)} %get-tuple-element.222) | copy-start | bytes 589828
  200.2 8.1 %copy-start.4 = (bf16[2048,3,48]{0,2,1:T(8,128)(2,1)S(1)}, bf16[2048,3,48]{0,2,1:T(8,128)(2,1)}, u32[]{:S(2)}) copy-start(bf16[2048,3,48]{0,2,1:T(8,128)(2,1)} %copy-done.3) | copy-start | bytes 1769476
  235.1 143.1 %reduce-scatter.20.cloned.1.call-start = ((), (), s32[]{:S(2)}) async-start(), calls=%async_computation.15 | async-start | bytes 2211840
  247.3 24.9 %copy-start.82 = (f32[768]{0:T(1024)S(1)}, f32[768]{0:T(1024)}, u32[]{:S(2)}) copy-start(f32[768]{0:T(1024)} %convert_element_type.83) | copy-start | bytes 9220
  250.2 29.2 %copy-start.8 = (f32[2048,3,64]{0,2,1:T(8,128)S(1)}, f32[2048,3,64]{0,2,1:T(8,128)}, u32[]{:S(2)}) copy-start(f32[2048,3,64]{0,2,1:T(8,128)} %copy-done.7) | copy-start | bytes 4718596
  250.2 29.2 %copy-start.11 = (f32[2048,3,64]{0,2,1:T(8,128)S(1)}, f32[2048,3,64]{0,2,1:T(8,128)}, u32[]{:S(2)}) copy-start(f32[2048,3,64]{0,2,1:T(8,128)} %copy-done.10) | copy-start | bytes 4718596
  250.2 342.2 %reduce-scatter.14.cloned.1.call-start = ((), (), s32[]{:S(2)}) async-start(), calls=%async_computation.12 | async-start | bytes 15728640 | tf_op jit(solution)/shard_map/reduce_scatter | solution.py:216
  296.5 8.7 %copy-start.86 = (bf16[768,768]{1,0:T(8,128)(2,1)S(1)}, bf16[768,768]{1,0:T(8,128)(2,1)}, u32[]{:S(2)}) copy-start(bf16[768,768]{1,0:T(8,128)(2,1)} %all-gather.11.cloned.1.call-done) | copy-start | bytes 3538948
  320.7 387.0 %reduce-scatter.12.cloned.1.call-start = ((), (), s32[]{:S(2)}) async-start(), calls=%async_computation.10 | async-start | bytes 7864320 | tf_op jit(solution)/shard_map/reduce_scatter | solution.py:143
  330.3 424.0 %reduce-scatter.16.cloned.1.call-start = ((), (), s32[]{:S(2)}) async-start(), calls=%async_computation.13 | async-start | bytes 2654208 | tf_op jit(solution)/shard_map/reduce_scatter | solution.py:258
  337.3 8.5 %copy-start.93 = (f32[24]{0:T(128)S(1)}, f32[24]{0:T(128)}, u32[]{:S(2)}) copy-start(f32[24]{0:T(128)} %param.49) | copy-start | bytes 292
  337.3 463.2 %reduce-scatter.18.cloned.1.call-start = ((), (), s32[]{:S(2)}) async-start(), calls=%async_computation.14 | async-start | bytes 2654208 | tf_op jit(solution)/shard_map/reduce_scatter | solution.py:260
  344.3 248.1 %copy-start.2 = (f32[512,768]{1,0:T(8,128)S(1)}, f32[512,768]{1,0:T(8,128)}, u32[]{:S(2)}) copy-start(f32[512,768]{1,0:T(8,128)} %param.35) | copy-start | bytes 4718596
  344.3 248.1 %copy-start.67 = (f32[512]{0:T(512)S(1)}, f32[512]{0:T(512)}, u32[]{:S(2)}) copy-start(f32[512]{0:T(512)} %copy-done.66) | copy-start | bytes 6148
  344.3 248.1 %copy-start.70 = (f32[768]{0:T(1024)S(1)}, f32[768]{0:T(1024)}, u32[]{:S(2)}) copy-start(f32[768]{0:T(1024)} %copy-done.69) | copy-start | bytes 9220
  344.3 248.1 %copy-start.72 = (f32[768]{0:T(1024)S(1)}, f32[768]{0:T(1024)}, u32[]{:S(2)}) copy-start(f32[768]{0:T(1024)} %copy-done.71) | copy-start | bytes 9220
  344.3 248.1 %copy-start.74 = (f32[512]{0:T(512)S(1)}, f32[512]{0:T(512)}, u32[]{:S(2)}) copy-start(f32[512]{0:T(512)} %copy-done.73) | copy-start | bytes 6148
  346.0 18.9 %copy-start.75 = (f32[768]{0:T(1024)}, f32[768]{0:T(1024)S(1)}, u32[]{:S(2)}) copy-start(f32[768]{0:T(1024)S(1)} %dynamic-update-slice.27) | copy-start | bytes 9220
  363.2 344.4 %copy-start.6 = (f32[512,768]{1,0:T(8,128)S(1)}, f32[512,768]{1,0:T(8,128)}, u32[]{:S(2)}) copy-start(f32[512,768]{1,0:T(8,128)} %param.36) | copy-start | bytes 4718596
  380.0 215.5 %copy-start.76 = (f32[768]{0:T(1024)S(1)}, f32[768]{0:T(1024)}, u32[]{:S(2)}) copy-start(f32[768]{0:T(1024)} %copy-done.75) | copy-start | bytes 9220
  (64 other events, 216.1 us)
Sparse Core Ops, SparseCore 0:
  55.8 63.2 all-gather.6
  120.7 62.0 all-gather.14
  184.7 22.5 all-gather.10
  208.7 63.4 all-gather.8
  273.9 22.5 all-gather.12
  299.5 34.9 reduce-scatter.21
  337.9 40.2 reduce-scatter.19
  380.5 211.8 reduce-scatter.13
  594.7 112.8 reduce-scatter.11
  711.4 42.8 reduce-scatter.15
  758.2 42.3 reduce-scatter.17
where the time goes:
time: 813 us; the launch traced here: 808 us
  waiting for transfers between devices  433 us (53%)
  blocking collectives  150 us (18%)
  matrix products  127 us (16%)
  other arithmetic  49.9 us (6%)
  local copies, waits for them, and re-layouts  27.8 us (3%)
  between operations  17.8 us (2%)
    reduce_scatter x1, waiting for transfers between devices, shards(): lax.psum_scatter(jnp.concatenate([first, second], axis=1), 'tensor', scat...  212 us
    unnamed x4, blocking collectives  120 us
    reduce_scatter x1, waiting for transfers between devices, shards(): lax.psum_scatter(jnp.dot(attended_flat, full_proj, preferred_element_type...  59.1 us
    reduce_scatter x1, waiting for transfers between devices, shards(): lax.psum_scatter(down_grad, 'dp', scatter_dimension=1, tiled=True)  46.3 us
    reduce_scatter x1, waiting for transfers between devices, shards(): lax.psum_scatter(up_grad, 'dp', scatter_dimension=0, tiled=True)  42.7 us
    unnamed x227, local copies, waits for them, and re-layouts  25.9 us
    all_gather x1, waiting for transfers between devices, shards(): lax.all_gather(mixed_two.astype(jnp.bfloat16), 'tensor', axis=0, tiled=True)  21.9 us
    dot_general x4, matrix products, shards(): jnp.einsum('hqk,qhd->khd', probs.astype(jnp.bfloat16), block_grad, prefer...  19.1 us
  transfers between devices with their start and end apart: 11, of which 9 were waited for; matrix products, arithmetic and copies ran while one was open for 23% of the time, Pallas kernels for 0%

commit v1 on v0

v1 whole, which is shorter than its diff:
```python
import functools

import jax
import jax.numpy as jnp
from jax import lax
from jax.experimental import pallas as pl
from jax.experimental.pallas import tpu as pltpu
from jax.sharding import PartitionSpec as P

HD = 64
ROT = 16
EPSILON = 1e-05
NEGATIVE = -1e30
LANES = 128
BF = jnp.bfloat16
F32 = jnp.float32
ANY = pl.BlockSpec(memory_space=pl.ANY)
VMEM = pl.BlockSpec(memory_space=pltpu.VMEM)
VMEM_LIMIT = 60 * 1024 * 1024


def dot(a, b, ca, cb):
    return lax.dot_general(a, b, (((ca,), (cb,)), ((), ())), preferred_element_type=F32)


def flip(index, mask):
    out = index
    bit = 0
    while (1 << bit) <= mask:
        if (mask >> bit) & 1:
            step = 1 << bit
            out = out + (1 - 2 * ((index // step) % 2)) * step
        bit += 1
    return out


def span(bits):
    masks = [0]
    for bit in bits:
        masks = masks + [m | (1 << bit) for m in masks]
    return masks


def remote(src, dst, send_sem, recv_sem, device):
    return pltpu.make_async_remote_copy(
        src_ref=src,
        dst_ref=dst,
        send_sem=send_sem,
        recv_sem=recv_sem,
        device_id=device,
        device_id_type=pl.DeviceIdType.MESH,
    )


def shift_order(count):
    return sorted(range(1, count), key=lambda s: (min(s, count - s), s))


def gather_plan(count, places, arrays):
    nbits = count.bit_length() - 1
    first = list(range(nbits - 1, -1, -1))
    second = [first[1], first[0]] + first[2:] if nbits >= 3 else first
    chunks = []
    for a in range(arrays):
        for s in [0] + shift_order(places):
            chunks.append((a, s, (first, second)[len(chunks) % 2]))
    return nbits, chunks


def gather_kernel(
    count, places, arrays, w_ref, vec_ref, g_ref, vout_ref, zs, zr, ds, dr, vs, vr, ls
):
    me, mz = lax.axis_index("dp"), lax.axis_index("tensor")
    total = count * places

    def vec_copy(i, sending):
        di, zi = i // places, i % places
        if sending:
            slot = (me, mz)
        else:
            slot = ((me + count - di) % count, (mz + places - zi) % places)
        return remote(
            vec_ref,
            vout_ref.at[slot[0], slot[1]],
            vs.at[i],
            vr.at[i],
            ((me + di) % count, (mz + zi) % places),
        )

    def send_vec(i, carry):
        vec_copy(i, True).start()
        return carry

    lax.fori_loop(1, total, send_vec, 0)

    nbits, chunks = gather_plan(count, places, arrays)
    own = [
        pltpu.make_async_copy(w_ref.at[a], g_ref.at[a, mz, me], ls.at[a]) for a in range(arrays)
    ]
    own_vec = pltpu.make_async_copy(vec_ref, vout_ref.at[me, mz], ls.at[arrays])

    def z_copy(a, s, sending):
        slot = mz if sending else (mz + places - s) % places
        n = a * (places - 1) + s - 1
        return remote(
            w_ref.at[a],
            g_ref.at[a, slot, me],
            zs.at[n],
            zr.at[n],
            (me, (mz + s) % places),
        )

    def d_copies(j, k, sending):
        a, s, order = chunks[j]
        place = (mz + places - s) % places
        bit = order[k]
        out = []
        for i, m in enumerate(span(order[:k])):
            slot = flip(me, m if sending else m | (1 << bit))
            src = w_ref.at[a] if s == 0 and m == 0 and sending else g_ref.at[a, place, slot]
            n = j * (count - 1) + (1 << k) - 1 + i
            out.append(
                remote(
                    src,
                    g_ref.at[a, place, slot],
                    ds.at[n],
                    dr.at[n],
                    (flip(me, 1 << bit), mz),
                )
            )
        return out

    for a in range(arrays):
        for s in shift_order(places):
            z_copy(a, s, True).start()
    for copy in own:
        copy.start()
    own_vec.start()
    for slot in range(len(chunks) + nbits):
        for k in range(nbits, -1, -1):
            j = slot - k
            if not 0 <= j < len(chunks):
                continue
            if k == 0:
                if chunks[j][1] > 0:
                    z_copy(chunks[j][0], chunks[j][1], False).wait_recv()
            else:
                for copy in d_copies(j, k - 1, False):
                    copy.wait_recv()
            if k < nbits:
                for copy in d_copies(j, k, True):
                    copy.start()
    for copy in own:
        copy.wait()
    own_vec.wait()

    def wait_vec(i, carry):
        vec_copy(i, False).wait_recv()
        vec_copy(i, True).wait_send()
        return carry

    lax.fori_loop(1, total, wait_vec, 0)
    for a in range(arrays):
        for s in range(1, places):
            z_copy(a, s, True).wait_send()
    for j in range(len(chunks)):
        for k in range(nbits):
            for copy in d_copies(j, k, True):
                copy.wait_send()


def gather_all(weights, vector, count, places):
    arrays, rows, width = weights.shape
    chunks = arrays * places
    sem = pltpu.SemaphoreType.DMA
    return pl.pallas_call(
        functools.partial(gather_kernel, count, places, arrays),
        out_shape=(
            jax.ShapeDtypeStruct((arrays, places, count, rows, width), weights.dtype),
            jax.ShapeDtypeStruct((count, places) + vector.shape, vector.dtype),
        ),
        in_specs=[VMEM, VMEM],
        out_specs=(ANY, ANY),
        scratch_shapes=[
            sem((arrays * (places - 1),)),
            sem((arrays * (places - 1),)),
            sem((chunks * (count - 1),)),
            sem((chunks * (count - 1),)),
            sem((count * places,)),
            sem((count * places,)),
            sem((arrays + 1,)),
        ],
        compiler_params=pltpu.CompilerParams(has_side_effects=True),
        name="gather_all",
    )(weights, vector)


def exchange_kernel(places, x_ref, y_ref, stage, ss, rs, ls):
    me, mz = lax.axis_index("dp"), lax.axis_index("tensor")

    def copy(s, sending):
        to = (mz + s) % places
        slot = mz if sending else (mz + places - s) % places
        return remote(x_ref.at[to], y_ref.at[slot], ss.at[s], rs.at[s], (me, to))

    for s in shift_order(places)[::-1]:
        copy(s, True).start()
    inward = pltpu.make_async_copy(x_ref.at[mz], stage, ls.at[0])
    inward.start()
    inward.wait()
    outward = pltpu.make_async_copy(stage, y_ref.at[mz], ls.at[1])
    outward.start()
    outward.wait()
    for s in range(1, places):
        copy(s, False).wait_recv()
    for s in range(1, places):
        copy(s, True).wait_send()


def exchange(x, places):
    sem = pltpu.SemaphoreType.DMA
    return pl.pallas_call(
        functools.partial(exchange_kernel, places),
        out_shape=jax.ShapeDtypeStruct(x.shape, x.dtype),
        in_specs=[ANY],
        out_specs=ANY,
        scratch_shapes=[
            pltpu.VMEM(x.shape[1:], x.dtype),
            sem((places,)),
            sem((places,)),
            sem((2,)),
        ],
        compiler_params=pltpu.CompilerParams(has_side_effects=True),
        name="exchange",
    )(x)


def scatter_plan(count, places, arrays):
    nbits = count.bit_length() - 1
    first = list(range(nbits))
    second = [first[0], first[2], first[1]] + first[3:] if nbits >= 3 else first
    chunks = []
    for a in range(arrays):
        for s in shift_order(places)[::-1] + [0]:
            chunks.append((a, s, (first, second)[len(chunks) % 2]))
    return nbits, chunks


def add_rows(acc_ref, other_ref):
    rows = acc_ref.shape[0]
    step = 32 if rows % 32 == 0 else rows

    def body(i, carry):
        at = pl.ds(i * step, step)
        acc_ref[at, :] = (acc_ref[at, :].astype(F32) + other_ref[at, :].astype(F32)).astype(BF)
        return carry

    lax.fori_loop(0, rows // step, body, 0)


def scatter_kernel(count, places, arrays, *refs):
    nbits, chunks = scatter_plan(count, places, arrays)
    gr_ref, vec_ref, out_ref, vout_ref, acc = refs[:5]
    rbs = refs[5 : 5 + nbits]
    zb, vb, ks, kr, zs, zr, vs, vr, ls = refs[5 + nbits :]
    me, mz = lax.axis_index("dp"), lax.axis_index("tensor")
    total = count * places

    def vec_copy(i, sending):
        to = ((me + i // places) % count, (mz + i % places) % places)
        return remote(vec_ref.at[to[0], to[1]], vb.at[i], vs.at[i], vr.at[i], to)

    def send_vec(i, carry):
        vec_copy(i, True).start()
        return carry

    lax.fori_loop(1, total, send_vec, 0)
    own_vec = pltpu.make_async_copy(vec_ref.at[me, mz], vb.at[0], ls.at[0])
    own_vec.start()

    def loads(j):
        a, s, order = chunks[j]
        place = (mz + s) % places
        out = []
        for i, m in enumerate(span(order[1:])):
            n = 1 + j * (count // 2) + i
            out.append(
                pltpu.make_async_copy(gr_ref.at[a, place, flip(me, m)], acc.at[j, i], ls.at[n])
            )
        return out

    def copies(j, k):
        a, s, order = chunks[j]
        place = (mz + s) % places
        base = span(order[1:])
        out = []
        for i, m in enumerate(span(order[k + 1 :])):
            far = m | (1 << order[k])
            if k == 0:
                src = gr_ref.at[a, place, flip(me, far)]
            else:
                src = acc.at[j, base.index(far)]
            n = j * (count - 1) + (count - (count >> k)) + i
            out.append(
                remote(
                    src, rbs[k].at[j, i], ks.at[n], kr.at[n], (flip(me, 1 << order[k]), mz)
                )
            )
        return out

    def z_copy(j):
        a, s, _ = chunks[j]
        n = a * (places - 1) + s - 1
        return remote(acc.at[j, 0], zb.at[a, s - 1], zs.at[n], zr.at[n], (me, (mz + s) % places))

    for j in range(len(chunks)):
        for copy in copies(j, 0):
            copy.start()
        for copy in loads(j):
            copy.start()
    for slot in range(len(chunks) + nbits - 1):
        for k in range(nbits - 1, -1, -1):
            j = slot - k
            if not 0 <= j < len(chunks):
                continue
            _, s, order = chunks[j]
            base = span(order[1:])
            if k == 0:
                for copy in loads(j):
                    copy.wait()
            for i, (m, copy) in enumerate(zip(span(order[k + 1 :]), copies(j, k))):
                copy.wait_recv()
                add_rows(acc.at[j, base.index(m)], rbs[k].at[j, i])
            if k + 1 < nbits:
                for copy in copies(j, k + 1):
                    copy.start()
            elif s > 0:
                z_copy(j).start()

    own_vec.wait()

    def wait_vec(i, carry):
        vec_copy(i, False).wait_recv()
        vec_copy(i, True).wait_send()
        return carry

    lax.fori_loop(1, total, wait_vec, 0)
    vout_ref[...] = jnp.sum(vb[...], axis=0)
    for a in range(arrays):
        for j, (b, s, _) in enumerate(chunks):
            if b == a and s > 0:
                z_copy(j).wait_recv()
        for j, (b, s, _) in enumerate(chunks):
            if b == a and s == 0:
                result = acc[j, 0].astype(F32)
                for other in range(places - 1):
                    result = result + zb[a, other].astype(F32)
                out_ref[a] = result
    for j, (_, s, _) in enumerate(chunks):
        for k in range(nbits):
            for copy in copies(j, k):
                copy.wait_send()
        if s > 0:
            z_copy(j).wait_send()


def scatter_all(grads, vectors):
    arrays, places, count, rows, width = grads.shape
    nbits, chunks = scatter_plan(count, places, arrays)
    n = len(chunks)
    sem = pltpu.SemaphoreType.DMA
    return pl.pallas_call(
        functools.partial(scatter_kernel, count, places, arrays),
        out_shape=(
            jax.ShapeDtypeStruct((arrays, rows, width), F32),
            jax.ShapeDtypeStruct(vectors.shape[2:], F32),
        ),
        in_specs=[ANY, ANY],
        out_specs=(VMEM, VMEM),
        scratch_shapes=[pltpu.VMEM((n, count // 2, rows, width), BF)]
        + [pltpu.VMEM((n, count >> (k + 1), rows, width), BF) for k in range(nbits)]
        + [
            pltpu.VMEM((arrays, places - 1, rows, width), BF),
            pltpu.VMEM((count * places,) + vectors.shape[2:], F32),
            sem((n * (count - 1),)),
            sem((n * (count - 1),)),
            sem((arrays * (places - 1),)),
            sem((arrays * (places - 1),)),
            sem((count * places,)),
            sem((count * places,)),
            sem((1 + n * (count // 2),)),
        ],
        compiler_params=pltpu.CompilerParams(
            has_side_effects=True, vmem_limit_bytes=VMEM_LIMIT
        ),
        name="scatter_all",
    )(grads, vectors)


def turn_tiles(tiles, cosine, low, high):
    out = []
    for tile in tiles:
        ahead = pltpu.roll(tile, LANES - ROT // 2, 1)
        behind = pltpu.roll(tile, ROT // 2, 1)
        out.append(tile * cosine + ahead * low + behind * high)
    return out


def rotary_lanes(offsets):
    half = ROT // 2
    freq = 10000.0 ** (-(2.0 * jnp.arange(half, dtype=F32)) / ROT)
    angles = offsets.astype(F32)[:, None] * freq[None, :]
    cosine, sine = jnp.cos(angles), jnp.sin(angles)
    rows = offsets.shape[0]
    rest = jnp.zeros((rows, HD - ROT), F32)
    blank = jnp.zeros((rows, half), F32)
    one = jnp.concatenate([cosine, cosine, rest + 1.0], axis=1)
    low = jnp.concatenate([-sine, blank, rest], axis=1)
    high = jnp.concatenate([blank, sine, rest], axis=1)
    return tuple(jnp.concatenate([t, t], axis=1) for t in (one, low, high))


def project_kernel(wide, n1_ref, cot_ref, w_ref, b_ref, c_ref, lo_ref, hi_ref, x_ref):
    full = 3 * wide
    cut = full // LANES * LANES
    part = full - cut
    w = w_ref[0]
    forward = dot(n1_ref[...], w[:, : cut + LANES], 1, 0) + b_ref[0]
    backward = dot(cot_ref[...], w[:, cut:], 1, 0)
    turned = 2 * wide // LANES
    tiles = [forward[:, i * LANES : (i + 1) * LANES] for i in range(turned)]
    tiles = turn_tiles(tiles, c_ref[...], lo_ref[...], hi_ref[...])
    for i, tile in enumerate(tiles):
        x_ref[0, :, i * LANES : (i + 1) * LANES] = tile.astype(BF)
    x_ref[0, :, turned * LANES : cut] = forward[:, turned * LANES : cut].astype(BF)
    lane = lax.broadcasted_iota(jnp.int32, (forward.shape[0], LANES), 1)
    mixed = jnp.where(lane < part, forward[:, cut:], backward[:, :LANES])
    x_ref[0, :, cut : cut + LANES] = mixed.astype(BF)
    x_ref[0, :, cut + LANES :] = backward[:, LANES:].astype(BF)


def project(n1, cot, w, bias, tables, wide):
    places, model, width = w.shape
    rows = n1.shape[0]
    whole = pl.BlockSpec((rows, model), lambda z: (0, 0))
    table = pl.BlockSpec((rows, LANES), lambda z: (0, 0))
    return pl.pallas_call(
        functools.partial(project_kernel, wide),
        grid=(places,),
        out_shape=jax.ShapeDtypeStruct((places, rows, width), BF),
        in_specs=[
            whole,
            whole,
            pl.BlockSpec((1, model, width), lambda z: (z, 0, 0)),
            pl.BlockSpec((1, 1, bias.shape[2]), lambda z: (z, 0, 0)),
            table,
            table,
            table,
        ],
        out_specs=pl.BlockSpec((1, rows, width), lambda z: (z, 0, 0)),
        compiler_params=pltpu.CompilerParams(vmem_limit_bytes=VMEM_LIMIT),
        name="project",
    )(n1, cot, w, bias, *tables)


def attention_kernel(
    heads,
    block,
    y_ref,
    begin_ref,
    c_ref,
    lo_ref,
    hi_ref,
    r_ref,
    bias_ref,
    qh,
    kh,
    vh,
    oh,
    kt,
    vt,
    s_scr,
    dq,
    dk,
    dv,
):
    total = y_ref.shape[0]
    wide = heads * HD
    scale = HD**-0.5
    blocks = total // block

    def prepare(i, carry):
        at = pl.ds(pl.multiple_of(i * block, block), block)
        for h in range(heads):
            q = y_ref[at, h * HD : (h + 1) * HD].astype(F32) * scale
            k = y_ref[at, wide + h * HD : wide + (h + 1) * HD].astype(F32)
            v = y_ref[at, 2 * wide + h * HD : 2 * wide + (h + 1) * HD].astype(F32)
            qh[h, at, :] = q.astype(BF)
            kh[h, at, :] = k.astype(BF)
            vh[h, at, :] = v.astype(BF)
            oh[h, at, :] = y_ref[at, 3 * wide + h * HD : 3 * wide + (h + 1) * HD]
            kt[h, :, at] = k.T.astype(BF)
            vt[h, :, at] = v.T.astype(BF)
            dk[h, at, :] = jnp.zeros((block, HD), F32)
            dv[h, at, :] = jnp.zeros((block, HD), F32)
        return carry

    lax.fori_loop(0, blocks, prepare, 0)

    def row_block(i, carry):
        at = pl.ds(pl.multiple_of(i * block, block), block)
        begin = begin_ref[0:1, at]
        last = i * block + lax.broadcasted_iota(jnp.int32, (1, block), 1)
        queries = [qh[h, at, :] for h in range(heads)]
        grads = [oh[h, at, :] for h in range(heads)]

        def scores(j, peaks):
            keys = pl.ds(pl.multiple_of(j * block, block), block)
            place = j * block + lax.broadcasted_iota(jnp.int32, (block, block), 0)
            allowed = (place >= begin) & (place <= last)
            out = []
            for h in range(heads):
                s = dot(kh[h, keys, :], queries[h], 1, 1)
                s = jnp.where(allowed, s, NEGATIVE)
                s_scr[h, keys, :] = s
                out.append(jnp.maximum(peaks[h], jnp.max(s.reshape(block // 8, 8, block), axis=0)))
            return tuple(out)

        start = tuple(jnp.full((8, block), NEGATIVE, F32) for _ in range(heads))
        peaks = lax.fori_loop(0, i + 1, scores, start)
        peaks = [jnp.max(p, axis=0, keepdims=True) for p in peaks]

        def weigh(j, state):
            keys = pl.ds(pl.multiple_of(j * block, block), block)
            out = []
            for h in range(heads):
                mass, acc = state[h]
                p = jnp.exp(s_scr[h, keys, :] - peaks[h])
                s_scr[h, keys, :] = p
                mass = mass + jnp.sum(p.reshape(block // 8, 8, block), axis=0)
                acc = acc + dot(vt[h, :, keys], p.astype(BF), 1, 0)
                out.append((mass, acc))
            return tuple(out)

        start = tuple(
            (jnp.zeros((8, block), F32), jnp.zeros((HD, block), F32)) for _ in range(heads)
        )
        state = lax.fori_loop(0, i + 1, weigh, start)
        inverses, deltas = [], []
        for h in range(heads):
            mass = jnp.sum(state[h][0], axis=0, keepdims=True)
            inverse = 1.0 / mass
            attended = (state[h][1] * inverse).astype(BF).astype(F32)
            deltas.append(
                jnp.sum(attended * grads[h].astype(F32).T, axis=0, keepdims=True)
            )
            inverses.append(inverse)
            r_ref[at, 3 * wide + h * HD : 3 * wide + (h + 1) * HD] = attended.T.astype(BF)

        def back(j, acc):
            keys = pl.ds(pl.multiple_of(j * block, block), block)
            out = []
            for h in range(heads):
                p = s_scr[h, keys, :] * inverses[h]
                dv[h, keys, :] += dot(p.astype(BF), grads[h], 1, 0)
                g = dot(vh[h, keys, :], grads[h], 1, 1)
                ds = (p * (g - deltas[h])).astype(BF)
                dk[h, keys, :] += dot(ds, queries[h], 1, 0)
                out.append(acc[h] + dot(kt[h, :, keys], ds, 1, 0))
            return tuple(out)

        start = tuple(jnp.zeros((HD, block), F32) for _ in range(heads))
        acc = lax.fori_loop(0, i + 1, back, start)
        for h in range(heads):
            dq[h, at, :] = (acc[h] * scale).T
        return carry

    lax.fori_loop(0, blocks, row_block, 0)

    def finish(i, sums):
        at = pl.ds(pl.multiple_of(i * block, block), block)
        pieces = [d[h, at, :] for d in (dq, dk, dv) for h in range(heads)]
        out = []
        turned = 2 * wide // LANES
        for t in range(3 * wide // LANES + 1):
            if 2 * t + 1 < len(pieces):
                tile = jnp.concatenate(pieces[2 * t : 2 * t + 2], axis=1)
            else:
                tile = pieces[2 * t]
            if t < turned:
                tile = turn_tiles([tile], c_ref[at, :], -lo_ref[at, :], -hi_ref[at, :])[0]
            width = tile.shape[1]
            r_ref[at, t * LANES : t * LANES + width] = tile.astype(BF)
            out.append(sums[t] + jnp.sum(tile.reshape(block // 8, 8, width), axis=0))
        return tuple(out)

    start = []
    for t in range(3 * wide // LANES + 1):
        width = min(LANES, 3 * wide - t * LANES)
        start.append(jnp.zeros((8, width), F32))
    sums = lax.fori_loop(0, blocks, finish, tuple(start))
    for t, value in enumerate(sums):
        bias_ref[0:1, t * LANES : t * LANES + value.shape[1]] = jnp.sum(
            value, axis=0, keepdims=True
        )


def attention(y, begin, tables, heads):
    total, width = y.shape
    block = min(256, total)
    scratch = pltpu.VMEM
    return pl.pallas_call(
        functools.partial(attention_kernel, heads, block),
        out_shape=(
            jax.ShapeDtypeStruct((total, width), BF),
            jax.ShapeDtypeStruct((1, 3 * heads * HD), F32),
        ),
        in_specs=[VMEM] * 5,
        out_specs=(VMEM, VMEM),
        scratch_shapes=[scratch((heads, total, HD), BF)] * 4
        + [scratch((heads, HD, total), BF)] * 2
        + [scratch((heads, total, block), F32)]
        + [scratch((heads, total, HD), F32)] * 3,
        compiler_params=pltpu.CompilerParams(vmem_limit_bytes=VMEM_LIMIT),
        name="attention",
    )(y, begin, *tables)


def feed_kernel(
    n2_ref, n2t_ref, cot_ref, cott_ref, up_ref, down_ref, b_ref, out_ref, back_ref, gu_ref, gd_ref, gb_ref
):
    @pl.when(pl.program_id(0) == 0)
    def _():
        out_ref[...] = jnp.zeros_like(out_ref)
        back_ref[...] = jnp.zeros_like(back_ref)

    up, down = up_ref[0, 0], down_ref[0, 0]
    pre = dot(n2_ref[...], up, 1, 0) + b_ref[0]
    bell = 0.5 * (1.0 + lax.erf(pre * 0.7071067811865476))
    activ = (pre * bell).astype(BF)
    out_ref[...] += dot(activ, down, 1, 1)
    gd_ref[0] = dot(cott_ref[...], activ, 1, 0).astype(BF)
    slope = bell + pre * jnp.exp(-0.5 * pre * pre) * 0.3989422804014327
    grad = dot(cot_ref[...], down, 1, 0) * slope
    gb_ref[0] = jnp.sum(grad, axis=0, keepdims=True)
    grad = grad.astype(BF)
    gu_ref[0] = dot(n2t_ref[...], grad, 1, 0).astype(BF)
    back_ref[...] += dot(grad, up, 1, 1)


def feed(n2, cot, w, bias):
    places, model, width = w.shape[1:]
    rows = n2.shape[0]
    whole = pl.BlockSpec((rows, model), lambda z: (0, 0))
    turned = pl.BlockSpec((model, rows), lambda z: (0, 0))
    square = pl.BlockSpec((1, model, width), lambda z: (z, 0, 0))
    return pl.pallas_call(
        feed_kernel,
        grid=(places,),
        out_shape=(
            jax.ShapeDtypeStruct((rows, model), F32),
            jax.ShapeDtypeStruct((rows, model), F32),
            jax.ShapeDtypeStruct((places, model, width), BF),
            jax.ShapeDtypeStruct((places, model, width), BF),
            jax.ShapeDtypeStruct((places, 1, width), F32),
        ),
        in_specs=[
            whole,
            turned,
            whole,
            turned,
            pl.BlockSpec((1, 1, model, width), lambda z: (1, z, 0, 0)),
            pl.BlockSpec((1, 1, model, width), lambda z: (2, z, 0, 0)),
            pl.BlockSpec((1, 1, width), lambda z: (z, 0, 0)),
        ],
        out_specs=(
            whole,
            whole,
            square,
            square,
            pl.BlockSpec((1, 1, width), lambda z: (z, 0, 0)),
        ),
        compiler_params=pltpu.CompilerParams(vmem_limit_bytes=VMEM_LIMIT),
        name="feed",
    )(n2, n2.T, cot, cot.T, w, w, bias)


def return_kernel(wide, n1t_ref, cott_ref, z_ref, w_ref, out_ref, back_ref, g_ref):
    @pl.when(pl.program_id(0) == 0)
    def _():
        out_ref[...] = jnp.zeros_like(out_ref)
        back_ref[...] = jnp.zeros_like(back_ref)

    full = 3 * wide
    cut = full // LANES * LANES
    part = full - cut
    z, w = z_ref[0], w_ref[0]
    lane = lax.broadcasted_iota(jnp.int32, (z.shape[0], LANES), 1)
    middle = z[:, cut : cut + LANES]
    none = jnp.zeros_like(middle)
    ours = jnp.where(lane < part, middle, none)
    theirs = jnp.where(lane < part, none, middle)
    back_ref[...] += dot(
        jnp.concatenate([z[:, :cut], ours], axis=1), w[:, : cut + LANES], 1, 1
    )
    out_ref[...] += dot(
        jnp.concatenate([theirs, z[:, cut + LANES :]], axis=1), w[:, cut:], 1, 1
    )
    first = dot(n1t_ref[...], z[:, : cut + LANES], 1, 0)
    second = dot(cott_ref[...], z[:, cut:], 1, 0)
    lane = lax.broadcasted_iota(jnp.int32, (first.shape[0], LANES), 1)
    g_ref[0, :, :cut] = first[:, :cut].astype(BF)
    g_ref[0, :, cut : cut + LANES] = jnp.where(
        lane < part, first[:, cut:], second[:, :LANES]
    ).astype(BF)
    g_ref[0, :, cut + LANES :] = second[:, LANES:].astype(BF)


def returning(n1, cot, z, w, wide):
    places, rows, width = z.shape
    model = n1.shape[1]
    turned = pl.BlockSpec((model, rows), lambda z: (0, 0))
    whole = pl.BlockSpec((rows, model), lambda z: (0, 0))
    return pl.pallas_call(
        functools.partial(return_kernel, wide),
        grid=(places,),
        out_shape=(
            jax.ShapeDtypeStruct((rows, model), F32),
            jax.ShapeDtypeStruct((rows, model), F32),
            jax.ShapeDtypeStruct((places, model, width), BF),
        ),
        in_specs=[
            turned,
            turned,
            pl.BlockSpec((1, rows, width), lambda z: (z, 0, 0)),
            pl.BlockSpec((1, model, width), lambda z: (z, 0, 0)),
        ],
        out_specs=(whole, whole, pl.BlockSpec((1, model, width), lambda z: (z, 0, 0))),
        compiler_params=pltpu.CompilerParams(vmem_limit_bytes=VMEM_LIMIT),
        name="returning",
    )(n1.T, cot.T, z, w)


def norm_back(grad_out, normal, inverse, gain):
    scaled = grad_out * gain
    return inverse * (
        scaled
        - jnp.mean(scaled, axis=1, keepdims=True)
        - normal * jnp.mean(scaled * normal, axis=1, keepdims=True)
    )


def lanes(values, width=LANES):
    return jnp.pad(values, [(0, 0)] * (values.ndim - 1) + [(0, width - values.shape[-1])])


def shards(
    count,
    places,
    block_input,
    cotangent,
    segment_ids,
    token_offset,
    first_gain,
    first_shift,
    second_gain,
    second_shift,
    qkv_weight,
    qkv_bias,
    proj_weight,
    up_weight,
    up_bias,
    down_weight,
    out_bias,
):
    rows, model = block_input.shape
    depth = qkv_weight.shape[1]
    wide = qkv_weight.shape[2]
    heads = wide // HD
    ff = up_weight.shape[1]
    piece = first_gain.shape[0]
    total = segment_ids.shape[0]
    place = lax.axis_index("tensor")

    attn = jnp.concatenate([qkv_weight[0], qkv_weight[1], qkv_weight[2], proj_weight.T], axis=1)
    packed = jnp.stack([attn, up_weight, down_weight.T])
    vector = jnp.stack(
        [lanes(v) for v in (first_gain, first_shift, second_gain, second_shift, out_bias)]
        + [lanes(qkv_bias.astype(F32).reshape(-1)), lanes(up_bias.astype(F32))]
        + [jnp.zeros((LANES,), F32)]
    )
    weights, vectors = gather_all(packed, vector, count, places)
    weights = weights.reshape(3, places, model, ff)
    small = vectors[:, :, :5, :piece].transpose(2, 0, 1, 3).reshape(5, model)
    gain_one, shift_one, gain_two, shift_two, bias_out = (small[i] for i in range(5))
    bias_qkv = (
        vectors[:, :, 5, : 3 * wide // count]
        .reshape(count, places, 3, wide // count)
        .transpose(1, 2, 0, 3)
        .reshape(places, 1, 3 * wide)
    )
    cut = 3 * wide // LANES * LANES
    bias_qkv = lanes(bias_qkv, cut + LANES)
    bias_up = vectors[:, :, 6, : ff // count].transpose(1, 0, 2).reshape(places, 1, ff)

    center = block_input - jnp.mean(block_input, axis=1, keepdims=True)
    inverse = lax.rsqrt(jnp.mean(center * center, axis=1, keepdims=True) + EPSILON)
    normal = center * inverse
    n1 = (normal * gain_one + shift_one).astype(BF)
    n2 = (normal * gain_two + shift_two).astype(BF)
    cot = cotangent.astype(BF)

    tables = rotary_lanes(token_offset)
    mine = tuple(lax.dynamic_slice_in_dim(t, place * rows, rows, 0) for t in tables)
    x = project(n1, cot, weights[0], bias_qkv, mine, wide)
    y = exchange(x, places)
    begin = (jnp.arange(total, dtype=jnp.int32) - token_offset)[None, :]
    r, qkv_bias_part = attention(y.reshape(total, y.shape[2]), begin, tables, heads)
    z = exchange(r.reshape(places, rows, r.shape[1]), places)
    out_two, grad_two, up_grad, down_grad, up_bias_part = feed(n2, cot, weights, bias_up)
    out_one, grad_one, attn_grad = returning(n1, cot, z, weights[0], wide)

    block_output = block_input + (out_one + out_two) + bias_out
    input_grad = (
        cotangent
        + norm_back(grad_one, normal, inverse, gain_one)
        + norm_back(grad_two, normal, inverse, gain_two)
    )
    sums = jnp.stack(
        [
            jnp.sum(grad_one * normal, axis=0),
            jnp.sum(grad_one, axis=0),
            jnp.sum(grad_two * normal, axis=0),
            jnp.sum(grad_two, axis=0),
            jnp.sum(cotangent, axis=0),
        ]
    )
    sums = lanes(sums.reshape(5, count, places, piece).transpose(1, 2, 0, 3))
    qkv_sum = qkv_bias_part.reshape(3, count, wide // count).transpose(1, 0, 2)
    qkv_sum = lanes(qkv_sum.reshape(count, 1, 3 * wide // count))
    here = jnp.arange(places, dtype=jnp.int32)[None, :, None, None] == place
    qkv_sum = jnp.where(here, qkv_sum[:, None], 0.0)
    up_sum = lanes(up_bias_part.reshape(places, count, ff // count).transpose(1, 0, 2))[:, :, None]
    parts = jnp.concatenate([sums, qkv_sum, up_sum, jnp.zeros_like(up_sum)], axis=2)

    grads = jnp.stack([attn_grad, up_grad, down_grad]).reshape(3, places, count, depth, ff)
    done, vec = scatter_all(grads, parts)
    attn_done = done[0]
    qkv_weight_grad = jnp.stack([attn_done[:, i * wide : (i + 1) * wide] for i in range(3)])
    return (
        block_output,
        input_grad,
        vec[0, :piece],
        vec[1, :piece],
        vec[2, :piece],
        vec[3, :piece],
        qkv_weight_grad,
        vec[5, : 3 * wide // count].reshape(3, wide // count),
        attn_done[:, 3 * wide :].T,
        done[1],
        vec[6, : ff // count],
        done[2].T,
        vec[4, :piece],
    )


def solution(mesh):
    both = P(("dp", "tensor"))
    return jax.shard_map(
        functools.partial(shards, mesh.shape["dp"], mesh.shape["tensor"]),
        mesh=mesh,
        in_specs=(
            P(("dp", "tensor"), None),
            P(("dp", "tensor"), None),
            P("dp"),
            P("dp"),
            both,
            both,
            both,
            both,
            P(None, "dp", "tensor"),
            P(None, ("tensor", "dp")),
            P("tensor", "dp"),
            P("dp", "tensor"),
            P(("tensor", "dp")),
            P("tensor", "dp"),
            both,
        ),
        out_specs=(
            P(("dp", "tensor"), None),
            P(("dp", "tensor"), None),
            both,
            both,
            both,
            both,
            P(None, "dp", "tensor"),
            P(None, ("tensor", "dp")),
            P("tensor", "dp"),
            P("dp", "tensor"),
            P(("tensor", "dp")),
            P("tensor", "dp"),
            both,
        ),
        check_vma=False,
    )
```

time: 813 us -> 591 us (0.73)
  Pallas kernels: 0 us -> 498 us
  waiting for transfers between devices: 433 us -> 0 us
  blocking collectives: 150 us -> 0 us
  matrix products: 127 us -> 0 us
  local copies, waits for them, and re-layouts: 27.8 us -> 56.2 us
  between operations: 17.8 us -> 1.19 us
  other arithmetic: 49.9 us -> 34.3 us
    pallas_call x0 -> x8, Pallas kernels: none -> 498 us  [the longest x2 137 us: exchange(): pl.pallas_call(functools.partial(exchange_kernel, places), out_shape=jax....]
    reduce_scatter x4 -> x0, waiting for transfers between devices: 360 us -> none  [the longest x1 212 us: shards(): lax.psum_scatter(jnp.concatenate([first, second], axis=1), 'tensor', scat...]
    dot_general x34 -> x0, matrix products: 121 us -> none  [the longest x4 19.1 us: shards(): jnp.einsum('hqk,qhd->khd', probs.astype(jnp.bfloat16), block_grad, prefer...]
    unnamed x4 -> x0, blocking collectives: 120 us -> none
    all_gather x5 -> x0, waiting for transfers between devices: 57.7 us -> none  [the longest x1 21.9 us: shards(): lax.all_gather(mixed_two.astype(jnp.bfloat16), 'tensor', axis=0, tiled=True)]
    all_gather x3 -> x0, blocking collectives: 30.4 us -> none  [the longest x1 12.9 us: shards(): lax.all_gather(qkv_weight, 'dp', axis=1, tiled=True)]
    unnamed x227 -> x41, local copies, waits for them, and re-layouts: 25.9 us -> 7.18 us
    unnamed x13 -> x0, waiting for transfers between devices: 15 us -> none
  transfers between devices with their start and end apart: 11 -> 0, of which waited for: 9 -> 0; matrix products, arithmetic and copies ran while one was open for 23% -> 0% of each run, Pallas kernels for 0% -> 0%
where the time goes in v1:
time: 591 us; the launch traced here: 590 us
  Pallas kernels  498 us (84%)
  local copies, waits for them, and re-layouts  56.2 us (10%)
  other arithmetic  34.3 us (6%)
    pallas_call x2, Pallas kernels, exchange(): pl.pallas_call(functools.partial(exchange_kernel, places), out_shape=jax....  137 us
    pallas_call x1, Pallas kernels, scatter_all(): pl.pallas_call(functools.partial(scatter_kernel, count, places, arrays),...  135 us
    pallas_call x1, Pallas kernels, gather_all(): pl.pallas_call(functools.partial(gather_kernel, count, places, arrays), o...  122 us
    pallas_call x1, Pallas kernels, attention(): pl.pallas_call(functools.partial(attention_kernel, heads, block), out_sha...  64 us
    pallas_call x1, Pallas kernels, feed(): pl.pallas_call(feed_kernel, grid=(places,), out_shape=(jax.ShapeDtypeStru...  21.3 us
    concatenate x3, local copies, waits for them, and re-layouts, rotary_lanes(): return tuple((jnp.concatenate([t, t], axis=1) for t in (one, low, high)))  14.5 us

profile of v1, /device:TPU:0, one launch (start us, length us, event | category | flops | bytes accessed | tf_op | source)
XLA Modules:
  0.0 589.8 jit_solution(15803467729141150359)
XLA Ops:
  0.7 1.0 copy.64
  1.7 0.9 slice_bitcast_fusion.10
  2.7 1.8 pad_maximum_fusion.1.w_ref
  4.7 0.6 stack.97.vec_ref
  5.3 122.2 %gather_all.1 = (bf16[3,4,8,96,768]{4,3,2,1,0:T(8,128)(2,1)}, f32[8,4,8,128]{3,2,1,0:T(8,128)}) custom-call(bf16[3,96,768]{2,1,0:T(8,128)(2,1)} %pad_maximum_fusion.1.w_ref, f32[8,128]{1,0:T(8,128)} %stack.97.vec_ref), custom_call_target="tpu_custom_call" | custom-call | tf_op jit(solution)/shard_map/gather_all/pallas_call | solution.py:176
  127.5 0.9 slice_bitcast_fusion.3
  129.9 1.7 add_convert_fusion
  131.6 1.9 copy.65
  133.5 1.1 convert_bitcast_fusion.cott_ref
  134.6 2.3 copy.69.n1_ref
  136.9 1.0 convert_element_type.33
  137.8 2.3 copy.70.cot_ref
  140.2 4.8 slice.91
  144.9 0.9 slice.92
  147.3 5.5 multiply_sine_fusion
  152.8 1.0 add.88
  153.9 4.5 concatenate.24.c_ref
  158.4 1.7 constant_dynamic-slice_fusion.2.c_ref
  160.1 1.0 broadcast_in_dim.46
  161.1 5.0 concatenate.26.hi_ref
  166.1 5.0 concatenate.25.lo_ref
  171.2 1.9 constant_dynamic-slice_fusion
  173.0 7.5 %project.1.x_ref = bf16[4,512,768]{2,1,0:T(8,128)(2,1)} custom-call(bf16[512,768]{1,0:T(8,128)(2,1)} %copy.69.n1_ref, bf16[512,768]{1,0:T(8,128)(2,1)} %copy.70.cot_ref, bf16[4,768,768]{2,1,0:T(8,128)(2,1)} %bitcast.93, f32[4,1,640]{2,1,0:T(1,128)} %pad.49.b_ref, f32[512,128]{1,0:T(8,128)} %constant_dynamic-slice_fusion.2.c_ref, ...), custom_call_target="tpu_custom_call" | custom-call | tf_op jit(solution)/shard_map/project/pallas_call | solution.py:447
  180.5 63.1 %exchange.2 = bf16[4,512,768]{2,1,0:T(8,128)(2,1)} custom-call(bf16[4,512,768]{2,1,0:T(8,128)(2,1)} %project.1.x_ref), custom_call_target="tpu_custom_call" | custom-call | tf_op jit(solution)/shard_map/exchange/pallas_call | solution.py:222
  243.6 64.0 %attention.1 = (bf16[2048,768]{1,0:T(8,128)(2,1)}, f32[1,576]{1,0:T(1,128)}) custom-call(bf16[2048,768]{1,0:T(8,128)(2,1)} %bitcast.95, s32[1,2048]{1,0:T(1,128)} %bitcast.111, f32[2048,128]{1,0:T(8,128)} %concatenate.24.c_ref, f32[2048,128]{1,0:T(8,128)} %concatenate.25.lo_ref, f32[2048,128]{1,0:T(8,128)} %concatenate.26.hi_ref), custom_call_target="tpu_custom_call" | custom-call | tf_op jit(solution)/shard_map/attention/pallas_call | solution.py:612
  307.6 74.1 %exchange.3.z_ref = bf16[4,512,768]{2,1,0:T(8,128)(2,1)} custom-call(bf16[4,512,768]{2,1,0:T(8,128)(2,1)} %bitcast.101), custom_call_target="tpu_custom_call" | custom-call | tf_op jit(solution)/shard_map/exchange/pallas_call | solution.py:222
  381.7 11.0 %returning.1 = (f32[512,768]{1,0:T(8,128)}, f32[512,768]{1,0:T(8,128)}, bf16[4,768,768]{2,1,0:T(8,128)(2,1)}) custom-call(bf16[768,512]{1,0:T(8,128)(2,1)} %bitcast.96, bf16[768,512]{1,0:T(8,128)(2,1)} %convert_bitcast_fusion.cott_ref, bf16[4,512,768]{2,1,0:T(8,128)(2,1)} %exchange.3.z_ref, bf16[4,768,768]{2,1,0:T(8,128)(2,1)} %bitcast.94), custom_call_target="tpu_custom_call" | custom-call | tf_op jit(solution)/shard_map/returning/pallas_call | solution.py:724
  392.7 1.2 copy.72.n2_ref
  393.9 0.9 slice.95
  394.8 0.7 reshape.140.b_ref
  395.5 21.3 %feed.1 = (f32[512,768]{1,0:T(8,128)}, f32[512,768]{1,0:T(8,128)}, bf16[4,768,768]{2,1,0:T(8,128)(2,1)}, bf16[4,768,768]{2,1,0:T(8,128)(2,1)}, f32[4,1,768]{2,1,0:T(1,128)}) custom-call(bf16[512,768]{1,0:T(8,128)(2,1)} %copy.72.n2_ref, bf16[768,512]{1,0:T(8,128)(2,1)} %bitcast.97, bf16[512,768]{1,0:T(8,128)(2,1)} %copy.70.cot_ref, ...), custom_call_target="tpu_custom_call" | custom-call | tf_op jit(solution)/shard_map/feed/pallas_call | solution.py:657
  416.9 3.3 add_add_fusion
  420.2 1.9 copy.76
  422.1 3.0 copy.74
  425.2 2.6 multiply_reduce_fusion
  427.8 2.0 multiply_add_fusion
  429.8 3.0 copy.81
  432.8 10.6 %pad_maximum_fusion.refs_0_ = bf16[3,4,8,96,768]{4,3,2,1,0:T(8,128)(2,1)} fusion(bf16[1,4,8,96,768]{4,3,2,1,0:T(8,128)(2,1)} %bitcast.100, bf16[1,4,8,96,768]{4,3,2,1,0:T(8,128)(2,1)} %bitcast.99, bf16[1,4,8,96,768]{4,3,2,1,0:T(8,128)(2,1)} %bitcast.98), kind=kLoop, calls=%fused_computation | loop fusion | flops 14155776 | bytes 28311552 | tf_op jit(solution)/shard_map/stack | solution.py:846
  443.9 1.7 reduce_sum.108
  446.6 0.7 fusion.2.refs_1_
  447.3 135.0 %scatter_all.1 = (f32[3,96,768]{2,1,0:T(8,128)}, f32[8,128]{1,0:T(8,128)}) custom-call(bf16[3,4,8,96,768]{4,3,2,1,0:T(8,128)(2,1)} %pad_maximum_fusion.refs_0_, f32[8,4,8,128]{3,2,1,0:T(8,128)} %fusion.2.refs_1_), custom_call_target="tpu_custom_call" | custom-call | tf_op jit(solution)/shard_map/scatter_all/pallas_call | solution.py:372
  582.3 1.4 slice_bitcast_fusion.11
  583.6 2.0 slice_bitcast_fusion
  585.8 0.7 pad_maximum_fusion.2
  586.5 0.7 slice_reduce_fusion.5
  587.2 0.7 reshape_squeeze.7
  587.8 0.7 copy.82
  588.6 1.2 slice_bitcast_fusion.12
  (88 shorter events, 4.7 us)
Async XLA Ops:
  0.6 128.2 %copy-start.2 = (f32[512,768]{1,0:T(8,128)S(1)}, f32[512,768]{1,0:T(8,128)}, u32[]{:S(2)}) copy-start(f32[512,768]{1,0:T(8,128)} %param.15) | copy-start | bytes 4718596
  0.7 3.8 copy-start.17
  0.7 3.8 copy-start.11
  0.7 3.8 copy-start.12
  0.7 3.9 copy-start.13
  0.7 3.9 copy-start.14
  0.7 4.0 copy-start.15
  0.7 3.9 copy-start.16
  133.5 3.4 copy-start
  140.1 6.5 %copy-start.9 = (s32[2048]{0:T(1024)S(1)}, s32[2048]{0:T(1024)}, u32[]{:S(2)}) copy-start(s32[2048]{0:T(1024)} %param.17) | copy-start | bytes 24580
  381.7 11.0 %copy-start.5 = (bf16[512,768]{0,1:T(8,128)(2,1)S(1)}, bf16[512,768]{0,1:T(8,128)(2,1)}, u32[]{:S(2)}) copy-start(bf16[512,768]{0,1:T(8,128)(2,1)} %get-tuple-element.94) | copy-start | bytes 2359300
  395.5 21.4 %copy-start.3 = (f32[512,768]{1,0:T(8,128)S(1)}, f32[512,768]{1,0:T(8,128)}, u32[]{:S(2)}) copy-start(f32[512,768]{1,0:T(8,128)} %param.15) | copy-start | bytes 4718596
  425.1 2.6 copy-start.1
  425.2 2.6 copy-start.4
  432.8 10.7 %copy-start.7 = (f32[512,768]{1,0:T(8,128)S(1)}, f32[512,768]{1,0:T(8,128)}, u32[]{:S(2)}) copy-start(f32[512,768]{1,0:T(8,128)} %get-tuple-element.32) | copy-start | bytes 4718596
  443.6 2.1 copy-start.6
  443.9 2.2 copy-start.8
  443.9 2.3 copy-start.10

commit v2 on v0

v2 whole, which is shorter than its diff:
```python
import functools

import jax
import jax.numpy as jnp
from jax import lax
from jax.experimental import pallas as pl
from jax.experimental.pallas import tpu as pltpu
from jax.sharding import PartitionSpec as P

HD = 64
ROT = 16
EPSILON = 1e-05
NEGATIVE = -1e30
LANES = 128
GROUP = 4 * HD
BF = jnp.bfloat16
F32 = jnp.float32
ANY = pl.BlockSpec(memory_space=pl.ANY)
VMEM = pl.BlockSpec(memory_space=pltpu.VMEM)
VMEM_LIMIT = 60 * 1024 * 1024


def dot(a, b, ca, cb):
    return lax.dot_general(a, b, (((ca,), (cb,)), ((), ())), preferred_element_type=F32)


def flip(index, mask):
    out = index
    bit = 0
    while (1 << bit) <= mask:
        if (mask >> bit) & 1:
            step = 1 << bit
            out = out + (1 - 2 * ((index // step) % 2)) * step
        bit += 1
    return out


def span(bits):
    masks = [0]
    for bit in bits:
        masks = masks + [m | (1 << bit) for m in masks]
    return masks


def remote(src, dst, send_sem, recv_sem, device):
    return pltpu.make_async_remote_copy(
        src_ref=src,
        dst_ref=dst,
        send_sem=send_sem,
        recv_sem=recv_sem,
        device_id=device,
        device_id_type=pl.DeviceIdType.MESH,
    )


def turn_tiles(tiles, cosine, low, high):
    out = []
    for tile in tiles:
        ahead = pltpu.roll(tile, LANES - ROT // 2, 1)
        behind = pltpu.roll(tile, ROT // 2, 1)
        out.append(tile * cosine + ahead * low + behind * high)
    return out


def rotary_turns(offsets):
    half = ROT // 2
    freq = 10000.0 ** (-(2.0 * jnp.arange(half, dtype=F32)) / ROT)
    angles = offsets.astype(F32)[None, :] * freq[:, None]
    return jnp.concatenate([jnp.cos(angles), jnp.sin(angles)], axis=0)


def spread_turns(turns):
    half = ROT // 2
    lane = lax.broadcasted_iota(jnp.int32, (ROT, LANES), 1) % HD
    line = lax.broadcasted_iota(jnp.int32, (ROT, LANES), 0)
    picks = (
        jnp.where((lane < ROT) & (line == lane % half), 1.0, 0.0),
        jnp.where((lane < half) & (line == half + lane), -1.0, 0.0),
        jnp.where((lane >= half) & (lane < ROT) & (line == lane), 1.0, 0.0),
    )
    tables = [
        lax.dot_general(
            turns,
            pick,
            (((0,), (0,)), ((), ())),
            precision=lax.Precision.HIGHEST,
            preferred_element_type=F32,
        )
        for pick in picks
    ]
    column = lax.broadcasted_iota(jnp.int32, tables[0].shape, 1) % HD
    tables[0] = jnp.where(column < ROT, tables[0], 1.0)
    return tables


def select_rows(values, pick, keep):
    spread = lax.dot_general(
        values,
        pick,
        (((1,), (0,)), ((), ())),
        precision=lax.Precision.HIGHEST,
        preferred_element_type=F32,
    )
    return jnp.where(keep, spread, 0.0)


def front_kernel(
    count,
    places,
    wide,
    piece,
    x_ref,
    cot_ref,
    w_ref,
    vec_ref,
    cs_ref,
    y_ref,
    p_ref,
    small_ref,
    out_ref,
    back_ref,
    gu_ref,
    gd_ref,
    gb_ref,
    g_ref,
    x_buf,
    n1_ref,
    n2_ref,
    cb_ref,
    n2t_ref,
    cbt_ref,
    table_ref,
    vb_ref,
    bq_ref,
    bu_ref,
    gu_buf,
    gd_buf,
    zs,
    zr,
    ds,
    dr,
    vs,
    vr,
    xs,
    xr,
    ls,
):
    me, mz = lax.axis_index("dp"), lax.axis_index("tensor")
    total = count * places
    rows, model = x_ref.shape
    ff = w_ref.shape[2]
    nbits = count.bit_length() - 1
    first = list(range(nbits - 1, -1, -1))
    second = [first[1], first[0]] + first[2:] if nbits >= 3 else first
    head_chunks = [(0, s, (first, second)[s % 2]) for s in range(places)]
    feed_chunks = [(a, s, (first, second)[a - 1]) for s in range(places) for a in (1, 2)]
    chunks = head_chunks + feed_chunks

    def vec_copy(i, sending):
        di, zi = i // places, i % places
        if sending:
            slot = me * places + mz
        else:
            slot = ((me + count - di) % count) * places + (mz + places - zi) % places
        return remote(
            vec_ref,
            vb_ref.at[slot],
            vs.at[i],
            vr.at[i],
            ((me + di) % count, (mz + zi) % places),
        )

    def z_copy(a, s, sending):
        slot = mz if sending else (mz + places - s) % places
        n = a * (places - 1) + s - 1
        return remote(
            w_ref.at[a], g_ref.at[a, slot, me], zs.at[n], zr.at[n], (me, (mz + s) % places)
        )

    def d_copies(j, k, sending):
        a, s, order = chunks[j]
        place = (mz + places - s) % places
        bit = order[k]
        out = []
        for i, m in enumerate(span(order[:k])):
            slot = flip(me, m if sending else m | (1 << bit))
            src = w_ref.at[a] if s == 0 and m == 0 and sending else g_ref.at[a, place, slot]
            n = j * (count - 1) + (1 << k) - 1 + i
            out.append(
                remote(
                    src,
                    g_ref.at[a, place, slot],
                    ds.at[n],
                    dr.at[n],
                    (flip(me, 1 << bit), mz),
                )
            )
        return out

    def step(j, k):
        a, s, _ = chunks[j]
        if k == 0:
            if s > 0:
                z_copy(a, s, False).wait_recv()
        else:
            for copy in d_copies(j, k - 1, False):
                copy.wait_recv()
        if k < nbits:
            for copy in d_copies(j, k, True):
                copy.start()

    def slot_steps(slot, low, high, lag, skip=()):
        for k in range(nbits, -1, -1):
            pair = slot - lag * k
            for j in (low + 2 * pair, low + 2 * pair + 1):
                if pair >= 0 and j < high and (j, k) not in skip:
                    step(j, k)

    def x_copy(h, s, sending):
        to = (mz + s) % places
        slot = mz if sending else (mz + places - s) % places
        n = h * places + s
        return remote(x_buf.at[to, h], y_ref.at[h, slot], xs.at[n], xr.at[n], (me, to))

    def keep_own(h):
        return pltpu.make_async_copy(x_buf.at[mz, h], y_ref.at[h, mz], ls.at[5 + h])

    own = [
        pltpu.make_async_copy(w_ref.at[a], g_ref.at[a, mz, me], ls.at[a]) for a in range(3)
    ]
    own_vec = pltpu.make_async_copy(vec_ref, vb_ref.at[me * places + mz], ls.at[3])

    def send_vec(i, carry):
        vec_copy(i, True).start()
        return carry

    lax.fori_loop(1, total, send_vec, 0)
    own_vec.start()
    heads_end = len(head_chunks)
    end = len(chunks)
    early = [(0, 0), (heads_end, 0), (heads_end + 1, 0)]
    for j, k in early:
        step(j, k)
    for a in range(3):
        for s in range(1, places):
            z_copy(a, s, True).start()
    for copy in own:
        copy.start()

    mine = cs_ref[:, pl.ds(pl.multiple_of(mz * rows, rows), rows)]
    for i, table in enumerate(spread_turns(mine)):
        table_ref[i] = table

    def wait_vec(i, carry):
        vec_copy(i, False).wait_recv()
        return carry

    own_vec.wait()
    lax.fori_loop(1, total, wait_vec, 0)
    values = vb_ref[...].reshape(total * 8, LANES)
    sub = lax.broadcasted_iota(jnp.int32, (total * 8, 1), 0)
    who, what = sub // 8, sub % 8
    which = lax.broadcasted_iota(jnp.int32, (LANES, 1), 0)

    def pick_of(at):
        return jnp.where(which == at, 1.0, 0.0)

    at = lax.broadcasted_iota(jnp.int32, (1, model), 1)
    kept = select_rows(values, pick_of(at % piece), who == at // piece)
    small_ref[...] = jnp.sum(kept.reshape(total, 8, model), axis=0)
    each = wide // count
    at = lax.broadcasted_iota(jnp.int32, (1, ff), 1)
    kind = at % GROUP // HD
    inner = at // GROUP * HD + at % HD
    kept = select_rows(
        values,
        pick_of(kind * each + inner % each),
        (what == 5) & (kind < 3) & (who // places == inner // each),
    )
    for z in range(places):
        bq_ref[z : z + 1, :] = jnp.sum(
            jnp.where(who % places == z, kept, 0.0), axis=0, keepdims=True
        )
    each = ff // count
    at = lax.broadcasted_iota(jnp.int32, (1, ff), 1)
    kept = select_rows(
        values, pick_of(at % each), (what == 6) & (who // places == at // each)
    )
    for z in range(places):
        bu_ref[z : z + 1, :] = jnp.sum(
            jnp.where(who % places == z, kept, 0.0), axis=0, keepdims=True
        )

    block = rows // 4

    def norm(i):
        here = slice(i * block, (i + 1) * block)
        values = x_ref[here, :]
        center = values - jnp.mean(values, axis=1, keepdims=True)
        inverse = lax.rsqrt(jnp.mean(center * center, axis=1, keepdims=True) + EPSILON)
        normal = center * inverse
        n1_ref[here, :] = (normal * small_ref[0:1, :] + small_ref[1:2, :]).astype(BF)
        second_norm = normal * small_ref[2:3, :] + small_ref[3:4, :]
        n2_ref[here, :] = second_norm.astype(BF)
        n2t_ref[:, here] = second_norm.astype(BF).astype(F32).T.astype(BF)
        cot = cot_ref[here, :]
        cb_ref[here, :] = cot.astype(BF)
        cbt_ref[:, here] = cot.T.astype(BF)

    slot_count = (heads_end + 1) // 2 + nbits
    for slot in range(slot_count):
        slot_steps(slot, 0, heads_end, 1, early)
        if slot < 4:
            norm(slot)
    for i in range(slot_count, 4):
        norm(i)
    own[0].wait()
    save = pltpu.make_async_copy(g_ref.at[0], p_ref, ls.at[4])
    save.start()

    lag = 2
    heads = ff // GROUP

    def project(i, carry):
        for slot in range(places):

            @pl.when(i == slot)
            def _():
                slot_steps(slot, heads_end, end, lag, early)

        to = (mz + 1 + i) % places
        w = g_ref[0, to].reshape(model, ff)
        forward = dot(n1_ref[...], w, 1, 0) + bq_ref[pl.ds(to, 1), :]
        column = lax.broadcasted_iota(jnp.int32, (rows, LANES), 1)
        for h in range(heads):
            tile = forward[:, h * GROUP : h * GROUP + LANES]
            tile = turn_tiles([tile], table_ref[0], table_ref[1], table_ref[2])[0]
            x_buf[to, h, :, :LANES] = tile.astype(BF)
            late = slice(h * GROUP + LANES, (h + 1) * GROUP)
            backward = dot(cb_ref[...], w[:, late], 1, 0)
            tile = jnp.where(column < HD, forward[:, late], backward)
            x_buf[to, h, :, LANES:] = tile.astype(BF)

        @pl.when(i < places - 1)
        def _():
            for h in range(heads):
                x_copy(h, 1 + i, True).start()

        @pl.when(i == places - 1)
        def _():
            for h in range(heads):
                keep_own(h).start()

        return carry

    lax.fori_loop(0, places, project, 0)

    out_ref[...] = jnp.zeros_like(out_ref)
    back_ref[...] = jnp.zeros_like(back_ref)
    own[1].wait()
    own[2].wait()
    width = ff // 2

    def puts(i):
        place = (mz + places - i) % places
        return [
            pltpu.make_async_copy(
                buf.at[i], ref.at[place], ls.at[5 + heads + 2 * i + a]
            )
            for a, (buf, ref) in enumerate(((gu_buf, gu_ref), (gd_buf, gd_ref)))
        ]

    def feed(f, carry):
        slot = places
        for i in range(places):
            until = i + lag * nbits

            @pl.when(f == 2 * i)
            def _(slot=slot, until=until):
                for t in range(slot, until + 1):
                    slot_steps(t, heads_end, end, lag, early)

            slot = max(slot, until + 1)
        i, h = f // 2, f % 2
        place = (mz + places - i) % places
        cols = pl.ds(pl.multiple_of(h * width, width), width)
        up = g_ref[1, place, :, :, cols].reshape(model, width)
        down = g_ref[2, place, :, :, cols].reshape(model, width)
        pre = dot(n2_ref[...], up, 1, 0) + bu_ref[pl.ds(place, 1), cols]
        bell = 0.5 * (1.0 + lax.erf(pre * 0.7071067811865476))
        activ = (pre * bell).astype(BF)
        out_ref[...] += dot(activ, down, 1, 1)
        gd_buf[i, :, cols] = dot(cbt_ref[...], activ, 1, 0).astype(BF)
        slope = bell + pre * jnp.exp(-0.5 * pre * pre) * 0.3989422804014327
        grad = dot(cb_ref[...], down, 1, 0) * slope
        gb_ref[pl.ds(place, 1), cols] = jnp.sum(grad, axis=0, keepdims=True)
        grad = grad.astype(BF)
        gu_buf[i, :, cols] = dot(n2t_ref[...], grad, 1, 0).astype(BF)
        back_ref[...] += dot(grad, up, 1, 1)

        @pl.when(h == 1)
        def _():
            for copy in puts(i):
                copy.start()

        return carry

    lax.fori_loop(0, 2 * places, feed, 0)

    save.wait()
    for i in range(places):
        for copy in puts(i):
            copy.wait()
    for h in range(heads):
        keep_own(h).wait()
        for s in range(1, places):
            x_copy(h, s, False).wait_recv()
        for s in range(1, places):
            x_copy(h, s, True).wait_send()

    def wait_sent(i, carry):
        vec_copy(i, True).wait_send()
        return carry

    lax.fori_loop(1, total, wait_sent, 0)
    for a in range(3):
        for s in range(1, places):
            z_copy(a, s, True).wait_send()
    for j in range(len(chunks)):
        for k in range(nbits):
            for copy in d_copies(j, k, True):
                copy.wait_send()


def front(block_input, cotangent, weights, vector, turns, count, places, wide, piece):
    rows, model = block_input.shape
    depth, ff = weights.shape[1:]
    total = count * places
    heads = ff // GROUP
    sem = pltpu.SemaphoreType.DMA
    shape = jax.ShapeDtypeStruct
    return pl.pallas_call(
        functools.partial(front_kernel, count, places, wide, piece),
        out_shape=(
            shape((heads, places, rows, GROUP), BF),
            shape((places, count, depth, ff), BF),
            shape((8, model), F32),
            shape((rows, model), F32),
            shape((rows, model), F32),
            shape((places, model, ff), BF),
            shape((places, model, ff), BF),
            shape((places, ff), F32),
        ),
        in_specs=[VMEM] * 5,
        out_specs=(ANY, ANY, VMEM, VMEM, VMEM, ANY, ANY, VMEM),
        scratch_shapes=[
            pltpu.VMEM((3, places, count, depth, ff), BF),
            pltpu.VMEM((places, heads, rows, GROUP), BF),
            pltpu.VMEM((rows, model), BF),
            pltpu.VMEM((rows, model), BF),
            pltpu.VMEM((rows, model), BF),
            pltpu.VMEM((model, rows), BF),
            pltpu.VMEM((model, rows), BF),
            pltpu.VMEM((3, rows, LANES), F32),
            pltpu.VMEM((total, 8, LANES), F32),
            pltpu.VMEM((places, ff), F32),
            pltpu.VMEM((places, ff), F32),
            pltpu.VMEM((places, model, ff), BF),
            pltpu.VMEM((places, model, ff), BF),
            sem((3 * (places - 1),)),
            sem((3 * (places - 1),)),
            sem((3 * places * (count - 1),)),
            sem((3 * places * (count - 1),)),
            sem((total,)),
            sem((total,)),
            sem((heads * places,)),
            sem((heads * places,)),
            sem((5 + heads + 2 * places,)),
        ],
        compiler_params=pltpu.CompilerParams(
            has_side_effects=True, vmem_limit_bytes=VMEM_LIMIT
        ),
        name="front",
    )(block_input, cotangent, weights, vector, turns)


class Scatter:
    def __init__(self, count, places, chunks, sources, acc, landing, sems, local):
        self.me, self.mz = lax.axis_index("dp"), lax.axis_index("tensor")
        self.count, self.places, self.chunks, self.sources = count, places, chunks, sources
        self.acc, self.landing, self.sems, self.local = acc, landing, sems, local
        self.nbits = count.bit_length() - 1

    @staticmethod
    def orders(count):
        nbits = count.bit_length() - 1
        first = list(range(nbits))
        return first, ([first[0], first[2], first[1]] + first[3:] if nbits >= 3 else first)

    def copies(self, j, k):
        a, s, order = self.chunks[j]
        to = (flip(self.me, 1 << order[k]), self.mz)
        half = self.count >> (k + 1)
        base = j * (half_of(self.count) + self.nbits - 1)
        send, recv = self.sems
        if k > 0:
            n = base + half_of(self.count) + k - 1
            src = self.acc.at[j, half : 2 * half]
            return [remote(src, self.landing[k].at[j], send.at[n], recv.at[n], to)]
        place = (self.mz + s) % self.places
        out = []
        for i, m in enumerate(span(order[1:][::-1])):
            slot = flip(self.me, m | (1 << order[0]))
            out.append(
                remote(
                    self.sources[a].at[place, slot],
                    self.landing[0].at[j, i],
                    send.at[base + i],
                    recv.at[base + i],
                    to,
                )
            )
        return out

    def loads(self, j):
        a, s, order = self.chunks[j]
        place = (self.mz + s) % self.places
        return [
            pltpu.make_async_copy(
                self.sources[a].at[place, flip(self.me, m)],
                self.acc.at[j, i],
                self.local.at[j * half_of(self.count) + i],
            )
            for i, m in enumerate(span(order[1:][::-1]))
        ]

    def start(self, j):
        for copy in self.copies(j, 0) + self.loads(j):
            copy.start()

    def stage(self, j, k, final=None):
        if k == 0:
            for copy in self.loads(j):
                copy.wait()
        for copy in self.copies(j, k):
            copy.wait_recv()
        half = self.count >> (k + 1)
        rows = self.acc.shape[2]
        step = 32 if rows % 32 == 0 else rows
        parts = rows // step
        target = self.acc.at[j] if final is None else final

        def body(i, carry):
            shard, at = i // parts, pl.ds(pl.multiple_of(i % parts * step, step), step)
            mine = self.acc[j, shard, at, :].astype(F32)
            other = self.landing[k][j, shard, at, :].astype(F32)
            target[shard, at, :] = (mine + other).astype(BF)
            return carry

        lax.fori_loop(0, half * parts, body, 0)
        if k + 1 < self.nbits:
            for copy in self.copies(j, k + 1):
                copy.start()

    def drain(self):
        for j in range(len(self.chunks)):
            for k in range(self.nbits):
                for copy in self.copies(j, k):
                    copy.wait_send()

    @staticmethod
    def scratch(count, chunks, rows, width):
        nbits = count.bit_length() - 1
        sem = pltpu.SemaphoreType.DMA
        copies = chunks * (half_of(count) + nbits - 1)
        return (
            [pltpu.VMEM((chunks, half_of(count), rows, width), BF)]
            + [pltpu.VMEM((chunks, count >> (k + 1), rows, width), BF) for k in range(nbits)]
            + [sem((copies,)), sem((copies,)), sem((chunks * half_of(count),))]
        )


def half_of(count):
    return count // 2


def middle_kernel(count, places, heads, wq, wk, *refs):
    y_ref, begin_ref, cs_ref, gu_ref, gd_ref, z_ref, bias_ref, red_ref = refs[:8]
    r_buf, qh, kh, vh, oh, kt, vt, s_scr, dq, dk, dv, at_scr, table_ref = refs[8:21]
    ss, rs, ls, acc = refs[21:25]
    nbits = count.bit_length() - 1
    landing = refs[25 : 25 + nbits]
    send, recv, local = refs[25 + nbits :]
    me, mz = lax.axis_index("dp"), lax.axis_index("tensor")
    total = y_ref.shape[1]
    rows = total // places
    scale = HD**-0.5
    nq = total // wq
    ratio = wq // wk

    chunks = []
    for s in list(range(1, places)) + [0]:
        for a in range(2):
            chunks.append((a, s, Scatter.orders(count)[a]))
    scatter = Scatter(
        count, places, chunks, (gu_ref, gd_ref), acc, landing, (send, recv), local
    )
    events = {}
    last_step = heads * nq
    for k in range(nbits):
        for pair in range(len(chunks) // 2):
            when = (2 + pair // 2, 5 + pair)[k] if k < 2 else 9 + pair + 4 * (k - 2)
            events.setdefault(min(when, last_step), []).append((pair, k))

    def run_events(step):
        for pair, k in events.get(step, []):
            for j in (2 * pair, 2 * pair + 1):
                a, s, _ = chunks[j]
                final = red_ref.at[a, pl.ds(s, 1)] if k == nbits - 1 else None
                scatter.stage(j, k, final)

    for j in range(len(chunks)):
        scatter.start(j)

    def tables(i, carry):
        at = pl.ds(pl.multiple_of(i * wk, wk), wk)
        cosine, low, high = spread_turns(cs_ref[:, at])
        table_ref[0, at, :] = cosine
        table_ref[1, at, :] = -low
        table_ref[2, at, :] = -high
        return carry

    lax.fori_loop(0, total // wk, tables, 0)

    def back_copy(h, s, sending):
        to = (mz + s) % places
        slot = mz if sending else (mz + places - s) % places
        n = h * places + s
        return remote(r_buf.at[h, to], z_ref.at[slot, h], ss.at[n], rs.at[n], (me, to))

    def keep_own(h):
        return pltpu.make_async_copy(r_buf.at[h, mz], z_ref.at[mz, h], ls.at[h])

    def flat(t, carry):
        h, i = t // nq, t % nq
        for step in sorted(events):
            if step < last_step:

                @pl.when(t == step)
                def _(step=step):
                    run_events(step)

        @pl.when(i == 0)
        def _():
            def prepare(b, carry):
                at = pl.ds(pl.multiple_of(b * wk, wk), wk)
                both = y_ref[h, at, :LANES].astype(F32)
                q, k = both[:, :HD] * scale, both[:, HD:]
                both = y_ref[h, at, LANES:].astype(F32)
                v, o = both[:, :HD], both[:, HD:]
                qh[at, :] = q.astype(BF)
                kh[at, :] = k.astype(BF)
                vh[at, :] = v.astype(BF)
                oh[at, :] = o.astype(BF)
                kt[:, at] = k.T.astype(BF)
                vt[:, at] = v.T.astype(BF)
                dk[at, :] = jnp.zeros((wk, HD), F32)
                dv[at, :] = jnp.zeros((wk, HD), F32)
                return carry

            lax.fori_loop(0, total // wk, prepare, 0)

        at = pl.ds(pl.multiple_of(i * wq, wq), wq)
        begin = begin_ref[0:1, at]
        last = i * wq + lax.broadcasted_iota(jnp.int32, (1, wq), 1)
        query, grad = qh[at, :], oh[at, :]
        trips = (i + 1) * ratio

        def scores(j, peak):
            keys = pl.ds(pl.multiple_of(j * wk, wk), wk)
            place = j * wk + lax.broadcasted_iota(jnp.int32, (wk, wq), 0)
            s = dot(kh[keys, :], query, 1, 1)
            s = jnp.where((place >= begin) & (place <= last), s, NEGATIVE)
            s_scr[keys, :] = s
            return jnp.maximum(peak, jnp.max(s.reshape(wk // 8, 8, wq), axis=0))

        peak = lax.fori_loop(0, trips, scores, jnp.full((8, wq), NEGATIVE, F32))
        peak = jnp.max(peak, axis=0, keepdims=True)

        def weigh(j, state):
            mass, out = state
            keys = pl.ds(pl.multiple_of(j * wk, wk), wk)
            p = jnp.exp(s_scr[keys, :] - peak)
            s_scr[keys, :] = p
            mass = mass + jnp.sum(p.reshape(wk // 8, 8, wq), axis=0)
            return mass, out + dot(vt[:, keys], p.astype(BF), 1, 0)

        mass, out = lax.fori_loop(
            0, trips, weigh, (jnp.zeros((8, wq), F32), jnp.zeros((HD, wq), F32))
        )
        inverse = 1.0 / jnp.sum(mass, axis=0, keepdims=True)
        attended = (out * inverse).astype(BF).astype(F32)
        delta = jnp.sum(attended * grad.astype(F32).T, axis=0, keepdims=True)
        at_scr[at, :] = attended.T

        def back(j, out):
            keys = pl.ds(pl.multiple_of(j * wk, wk), wk)
            p = s_scr[keys, :] * inverse
            dv[keys, :] += dot(p.astype(BF), grad, 1, 0)
            g = dot(vh[keys, :], grad, 1, 1)
            ds = (p * (g - delta)).astype(BF)
            dk[keys, :] += dot(ds, query, 1, 0)
            return out + dot(kt[:, keys], ds, 1, 0)

        out = lax.fori_loop(0, trips, back, jnp.zeros((HD, wq), F32))
        dq[at, :] = (out * scale).T

        @pl.when(i == nq - 1)
        def _():
            per = rows // wk

            def finish(b, sums):
                at = pl.ds(pl.multiple_of(b * wk, wk), wk)
                inside = pl.ds(pl.multiple_of(b % per * wk, wk), wk)
                tile = jnp.concatenate([dq[at, :], dk[at, :]], axis=1)
                tile = turn_tiles(
                    [tile], table_ref[0, at, :], table_ref[1, at, :], table_ref[2, at, :]
                )[0]
                r_buf[h, b // per, inside, :LANES] = tile.astype(BF)
                other = jnp.concatenate([dv[at, :], at_scr[at, :]], axis=1)
                r_buf[h, b // per, inside, LANES:] = other.astype(BF)
                return tuple(
                    total + jnp.sum(x.reshape(wk // 8, 8, LANES), axis=0)
                    for total, x in zip(sums, (tile, other))
                )

            zero = jnp.zeros((8, LANES), F32)
            sums = lax.fori_loop(0, total // wk, finish, (zero, zero))
            for c, value in enumerate(sums):
                bias_ref[h, :, c * LANES : (c + 1) * LANES] = value
            for s in range(1, places):
                back_copy(h, s, True).start()
            keep_own(h).start()

        return carry

    lax.fori_loop(0, last_step, flat, 0)
    run_events(last_step)
    for h in range(heads):
        keep_own(h).wait()
        for s in range(1, places):
            back_copy(h, s, False).wait_recv()
        for s in range(1, places):
            back_copy(h, s, True).wait_send()
    scatter.drain()


def middle(y, begin, turns, up_grad, down_grad):
    heads, total, group = y.shape
    places, count, depth, ff = up_grad.shape
    wq, wk = min(512, total), min(256, total)
    vmem = pltpu.VMEM
    sem = pltpu.SemaphoreType.DMA
    shape = jax.ShapeDtypeStruct
    return pl.pallas_call(
        functools.partial(middle_kernel, count, places, heads, wq, wk),
        out_shape=(
            shape((places, heads, total // places, group), BF),
            shape((heads, 8, group), F32),
            shape((2, places, depth, ff), BF),
        ),
        in_specs=[VMEM, VMEM, VMEM, ANY, ANY],
        out_specs=(ANY, VMEM, VMEM),
        scratch_shapes=[vmem((heads, places, total // places, group), BF)]
        + [vmem((total, HD), BF)] * 4
        + [vmem((HD, total), BF)] * 2
        + [vmem((total, wq), F32)]
        + [vmem((total, HD), F32)] * 4
        + [vmem((3, total, LANES), F32)]
        + [sem((heads * places,)), sem((heads * places,)), sem((heads,))]
        + Scatter.scratch(count, 2 * places, depth, ff),
        compiler_params=pltpu.CompilerParams(
            has_side_effects=True, vmem_limit_bytes=VMEM_LIMIT
        ),
        name="middle",
    )(y, begin, turns, up_grad, down_grad)


def return_kernel(n1t_ref, cb_ref, z_ref, w_ref, out_ref, back_ref, g_ref):
    @pl.when(pl.program_id(0) == 0)
    def _():
        out_ref[...] = jnp.zeros_like(out_ref)
        back_ref[...] = jnp.zeros_like(back_ref)

    heads = z_ref.shape[1]
    rows = z_ref.shape[2]
    model = w_ref.shape[1]
    left = lax.broadcasted_iota(jnp.int32, (rows, LANES), 1) < HD
    wide_left = lax.broadcasted_iota(jnp.int32, (model, LANES), 1) < HD
    out, back = out_ref[...], back_ref[...]
    for h in range(heads):
        z = z_ref[0, h]
        w = w_ref[0, :, h * GROUP : (h + 1) * GROUP]
        late = z[:, LANES:]
        none = jnp.zeros_like(late)
        ours = jnp.concatenate([z[:, :LANES], jnp.where(left, late, none)], axis=1)
        back = back + dot(ours, w, 1, 1)
        out = out + dot(jnp.where(left, none, late), w[:, LANES:], 1, 1)
        first = dot(n1t_ref[...], z, 1, 0)
        second = dot(cb_ref[...], late, 1, 0)
        g_ref[0, :, h * GROUP : h * GROUP + LANES] = first[:, :LANES].astype(BF)
        g_ref[0, :, h * GROUP + LANES : (h + 1) * GROUP] = jnp.where(
            wide_left, first[:, LANES:], second
        ).astype(BF)
    out_ref[...] = out
    back_ref[...] = back


def returning(n1, cot, z, w):
    places, heads, rows, group = z.shape
    model, width = w.shape[1:]
    turned = pl.BlockSpec((model, rows), lambda z: (0, 0))
    whole = pl.BlockSpec((rows, model), lambda z: (0, 0))
    square = pl.BlockSpec((1, model, width), lambda z: (z, 0, 0))
    return pl.pallas_call(
        return_kernel,
        grid=(places,),
        out_shape=(
            jax.ShapeDtypeStruct((rows, model), F32),
            jax.ShapeDtypeStruct((rows, model), F32),
            jax.ShapeDtypeStruct((places, model, width), BF),
        ),
        in_specs=[
            turned,
            turned,
            pl.BlockSpec((1, heads, rows, group), lambda z: (z, 0, 0, 0)),
            square,
        ],
        out_specs=(whole, whole, square),
        compiler_params=pltpu.CompilerParams(vmem_limit_bytes=VMEM_LIMIT),
        name="returning",
    )(n1.T, cot.T, z, w)


def last_kernel(count, places, *refs):
    g_ref, red_ref, vec_ref, out_ref, vout_ref, zb, vb, zs, zr, vs, vr, ls, acc = refs[:13]
    nbits = count.bit_length() - 1
    landing = refs[13 : 13 + nbits]
    send, recv, local = refs[13 + nbits :]
    me, mz = lax.axis_index("dp"), lax.axis_index("tensor")
    total = count * places

    def vec_copy(i, sending):
        to = ((me + i // places) % count, (mz + i % places) % places)
        return remote(vec_ref.at[to[0], to[1]], vb.at[i], vs.at[i], vr.at[i], to)

    def send_vec(i, carry):
        vec_copy(i, True).start()
        return carry

    chunks = []
    for i, s in enumerate(list(range(1, places)) + [0]):
        chunks.append((0, s, Scatter.orders(count)[i % 2]))
    scatter = Scatter(count, places, chunks, (g_ref,), acc, landing, (send, recv), local)
    for j in range(len(chunks)):
        scatter.start(j)

    def z_copy(a, s):
        n = a * (places - 1) + s - 1
        if a == 0:
            src = acc.at[s - 1, 0]
        else:
            src = red_ref.at[a - 1, s]
        return remote(src, zb.at[a, s - 1], zs.at[n], zr.at[n], (me, (mz + s) % places))

    for a in (1, 2):
        for s in range(1, places):
            z_copy(a, s).start()
    lax.fori_loop(1, total, send_vec, 0)
    own_vec = pltpu.make_async_copy(vec_ref.at[me, mz], vb.at[0], ls.at[0])
    own_vec.start()
    for slot in range((len(chunks) + 1) // 2 + nbits - 1):
        for k in range(nbits - 1, -1, -1):
            pair = slot - k
            for j in (2 * pair, 2 * pair + 1):
                if 0 <= pair and j < len(chunks):
                    scatter.stage(j, k)
                    if k == nbits - 1 and chunks[j][1] > 0:
                        z_copy(0, chunks[j][1]).start()
    own_vec.wait()

    def wait_vec(i, carry):
        vec_copy(i, False).wait_recv()
        vec_copy(i, True).wait_send()
        return carry

    lax.fori_loop(1, total, wait_vec, 0)
    vout_ref[...] = jnp.sum(vb[...], axis=0)
    for a in (1, 2, 0):
        for s in range(1, places):
            z_copy(a, s).wait_recv()
        own = acc[places - 1, 0] if a == 0 else red_ref[a - 1, 0]
        result = own.astype(F32)
        for s in range(1, places):
            result = result + zb[a, s - 1].astype(F32)
        out_ref[a] = result
    scatter.drain()
    for a in range(3):
        for s in range(1, places):
            z_copy(a, s).wait_send()


def scatter_last(grad, partly, vectors):
    places, count, rows, width = grad.shape
    total = count * places
    sem = pltpu.SemaphoreType.DMA
    return pl.pallas_call(
        functools.partial(last_kernel, count, places),
        out_shape=(
            jax.ShapeDtypeStruct((3, rows, width), F32),
            jax.ShapeDtypeStruct(vectors.shape[2:], F32),
        ),
        in_specs=[ANY, VMEM, ANY],
        out_specs=(VMEM, VMEM),
        scratch_shapes=[
            pltpu.VMEM((3, places - 1, rows, width), BF),
            pltpu.VMEM((total,) + vectors.shape[2:], F32),
            sem((3 * (places - 1),)),
            sem((3 * (places - 1),)),
            sem((total,)),
            sem((total,)),
            sem((1,)),
        ]
        + Scatter.scratch(count, places, rows, width),
        compiler_params=pltpu.CompilerParams(
            has_side_effects=True, vmem_limit_bytes=VMEM_LIMIT
        ),
        name="scatter_last",
    )(grad, partly, vectors)


def norm_back(grad_out, normal, inverse, gain):
    scaled = grad_out * gain
    return inverse * (
        scaled
        - jnp.mean(scaled, axis=1, keepdims=True)
        - normal * jnp.mean(scaled * normal, axis=1, keepdims=True)
    )


def lanes(values, width=LANES):
    return jnp.pad(values, [(0, 0)] * (values.ndim - 1) + [(0, width - values.shape[-1])])


def shards(
    count,
    places,
    block_input,
    cotangent,
    segment_ids,
    token_offset,
    first_gain,
    first_shift,
    second_gain,
    second_shift,
    qkv_weight,
    qkv_bias,
    proj_weight,
    up_weight,
    up_bias,
    down_weight,
    out_bias,
):
    rows, model = block_input.shape
    depth = qkv_weight.shape[1]
    wide = qkv_weight.shape[2]
    heads = wide // HD
    ff = up_weight.shape[1]
    piece = first_gain.shape[0]
    total = segment_ids.shape[0]
    place = lax.axis_index("tensor")

    attn = jnp.stack([qkv_weight[0], qkv_weight[1], qkv_weight[2], proj_weight.T])
    attn = attn.reshape(4, depth, heads, HD).transpose(1, 2, 0, 3).reshape(depth, 4 * wide)
    packed = jnp.stack([attn, up_weight, down_weight.T])
    vector = jnp.stack(
        [lanes(v) for v in (first_gain, first_shift, second_gain, second_shift, out_bias)]
        + [lanes(qkv_bias.astype(F32).reshape(-1)), lanes(up_bias.astype(F32))]
        + [jnp.zeros((LANES,), F32)]
    )
    turns = rotary_turns(token_offset)
    begin = (jnp.arange(total, dtype=jnp.int32) - token_offset)[None, :]
    y, attn_weights, small, out_two, grad_two, up_grad, down_grad, up_bias_part = front(
        block_input, cotangent, packed, vector, turns, count, places, wide, piece
    )
    attn_weights = attn_weights.reshape(places, model, ff)
    gain_one, shift_one, gain_two, shift_two, bias_out = (small[i] for i in range(5))
    z, qkv_bias_part, partly = middle(
        y.reshape(heads, total, GROUP),
        begin,
        turns,
        up_grad.reshape(places, count, depth, ff),
        down_grad.reshape(places, count, depth, ff),
    )
    center = block_input - jnp.mean(block_input, axis=1, keepdims=True)
    inverse = lax.rsqrt(jnp.mean(center * center, axis=1, keepdims=True) + EPSILON)
    normal = center * inverse
    n1 = (normal * gain_one + shift_one).astype(BF)
    out_one, grad_one, attn_grad = returning(n1, cotangent.astype(BF), z, attn_weights)

    block_output = block_input + (out_one + out_two) + bias_out
    input_grad = (
        cotangent
        + norm_back(grad_one, normal, inverse, gain_one)
        + norm_back(grad_two, normal, inverse, gain_two)
    )
    sums = jnp.stack(
        [
            jnp.sum(grad_one * normal, axis=0),
            jnp.sum(grad_one, axis=0),
            jnp.sum(grad_two * normal, axis=0),
            jnp.sum(grad_two, axis=0),
            jnp.sum(cotangent, axis=0),
        ]
    )
    sums = lanes(sums.reshape(5, count, places, piece).transpose(1, 2, 0, 3))
    qkv_sum = jnp.sum(qkv_bias_part, axis=1).reshape(heads, 4, HD)[:, :3].transpose(1, 0, 2)
    qkv_sum = qkv_sum.reshape(3, count, wide // count).transpose(1, 0, 2)
    qkv_sum = lanes(qkv_sum.reshape(count, 1, 3 * wide // count))
    here = jnp.arange(places, dtype=jnp.int32)[None, :, None, None] == place
    qkv_sum = jnp.where(here, qkv_sum[:, None], 0.0)
    up_sum = lanes(up_bias_part.reshape(places, count, ff // count).transpose(1, 0, 2))[:, :, None]
    parts = jnp.concatenate([sums, qkv_sum, up_sum, jnp.zeros_like(up_sum)], axis=2)

    done, vec = scatter_last(attn_grad.reshape(places, count, depth, ff), partly, parts)
    attn_done = done[0].reshape(depth, heads, 4, HD).transpose(2, 0, 1, 3).reshape(4, depth, wide)
    return (
        block_output,
        input_grad,
        vec[0, :piece],
        vec[1, :piece],
        vec[2, :piece],
        vec[3, :piece],
        attn_done[:3],
        vec[5, : 3 * wide // count].reshape(3, wide // count),
        attn_done[3].T,
        done[1],
        vec[6, : ff // count],
        done[2].T,
        vec[4, :piece],
    )


def solution(mesh):
    both = P(("dp", "tensor"))
    return jax.shard_map(
        functools.partial(shards, mesh.shape["dp"], mesh.shape["tensor"]),
        mesh=mesh,
        in_specs=(
            P(("dp", "tensor"), None),
            P(("dp", "tensor"), None),
            P("dp"),
            P("dp"),
            both,
            both,
            both,
            both,
            P(None, "dp", "tensor"),
            P(None, ("tensor", "dp")),
            P("tensor", "dp"),
            P("dp", "tensor"),
            P(("tensor", "dp")),
            P("tensor", "dp"),
            both,
        ),
        out_specs=(
            P(("dp", "tensor"), None),
            P(("dp", "tensor"), None),
            both,
            both,
            both,
            both,
            P(None, "dp", "tensor"),
            P(None, ("tensor", "dp")),
            P("tensor", "dp"),
            P("dp", "tensor"),
            P(("tensor", "dp")),
            P("tensor", "dp"),
            both,
        ),
        check_vma=False,
    )
```

time: 813 us -> 365 us (0.45)
  waiting for transfers between devices: 433 us -> 0 us
  Pallas kernels: 0 us -> 306 us
  blocking collectives: 150 us -> 0 us
  matrix products: 127 us -> 0 us
  other arithmetic: 49.9 us -> 27.5 us
  between operations: 17.8 us -> 0.88 us
    reduce_scatter x4 -> x0, waiting for transfers between devices: 360 us -> none  [the longest x1 212 us: shards(): lax.psum_scatter(jnp.concatenate([first, second], axis=1), 'tensor', scat...]
    pallas_call x0 -> x4, Pallas kernels: none -> 306 us  [the longest x1 128 us: middle(): pl.pallas_call(functools.partial(middle_kernel, count, places, heads, wq,...]
    dot_general x34 -> x0, matrix products: 121 us -> none  [the longest x4 19.1 us: shards(): jnp.einsum('hqk,qhd->khd', probs.astype(jnp.bfloat16), block_grad, prefer...]
    unnamed x4 -> x0, blocking collectives: 120 us -> none
    all_gather x5 -> x0, waiting for transfers between devices: 57.7 us -> none  [the longest x1 21.9 us: shards(): lax.all_gather(mixed_two.astype(jnp.bfloat16), 'tensor', axis=0, tiled=True)]
    all_gather x3 -> x0, blocking collectives: 30.4 us -> none  [the longest x1 12.9 us: shards(): lax.all_gather(qkv_weight, 'dp', axis=1, tiled=True)]
    unnamed x227 -> x21, local copies, waits for them, and re-layouts: 25.9 us -> 9.56 us
    unnamed x13 -> x0, waiting for transfers between devices: 15 us -> none
  transfers between devices with their start and end apart: 11 -> 0, of which waited for: 9 -> 0; matrix products, arithmetic and copies ran while one was open for 23% -> 0% of each run, Pallas kernels for 0% -> 0%
where the time goes in v2:
time: 365 us; the launch traced here: 364 us
  Pallas kernels  306 us (84%)
  local copies, waits for them, and re-layouts  29.3 us (8%)
  other arithmetic  27.5 us (8%)
    pallas_call x1, Pallas kernels, middle(): pl.pallas_call(functools.partial(middle_kernel, count, places, heads, wq,...  128 us
    pallas_call x1, Pallas kernels, front(): pl.pallas_call(functools.partial(front_kernel, count, places, wide, piece...  109 us
    pallas_call x1, Pallas kernels, scatter_last(): pl.pallas_call(functools.partial(last_kernel, count, places), out_shape=(...  54.1 us
    pallas_call x1, Pallas kernels, returning(): pl.pallas_call(return_kernel, grid=(places,), out_shape=(jax.ShapeDtypeSt...  14.4 us
    unnamed x21, local copies, waits for them, and re-layouts  9.56 us

profile of v2, /device:TPU:0, one launch (start us, length us, event | category | flops | bytes accessed | tf_op | source)
XLA Modules:
  0.0 363.6 jit_solution(12625431751438027115)
XLA Ops:
  0.7 0.8 reshape.126
  1.5 0.7 bitcast_convert_fusion
  2.1 0.7 pad_bitcast_fusion.1
  2.8 0.7 pad_bitcast_fusion.3
  3.5 0.7 pad_bitcast_fusion.5
  4.1 0.6 stack.81.vec_ref
  4.8 1.4 iota_subtract_fusion
  6.1 0.3 multiply_cosine_fusion
  6.5 0.7 pad_maximum_fusion.1.cs_ref.refs_2_
  7.1 1.1 copy.56
  8.2 0.8 maximum_bitcast_fusion
  9.1 0.1 copy.58
  9.2 0.8 pad_maximum_fusion.w_ref
  10.0 109.5 %front.1 = (bf16[3,4,512,256]{3,2,1,0:T(8,128)(2,1)}, bf16[4,8,96,768]{3,2,1,0:T(8,128)(2,1)}, f32[8,768]{1,0:T(8,128)}, f32[512,768]{1,0:T(8,128)}, f32[512,768...) custom-call(f32[512,768]{1,0:T(8,128)} %x_ref.1, ...), custom_call_target="tpu_custom_call" | custom-call | tf_op jit(solution)/shard_map/front/pallas_call | solution.py:442
  119.5 128.0 %middle.1 = (bf16[4,3,512,256]{3,2,1,0:T(8,128)(2,1)}, f32[3,8,256]{2,1,0:T(8,128)}, bf16[2,4,96,768]{3,2,1,0:T(8,128)(2,1)}) custom-call(bf16[3,2048,256]{2,1,0:T(8,128)(2,1)} %bitcast.76, s32[1,2048]{1,0:T(1,128)} %bitcast.90, f32[16,2048]{1,0:T(8,128)} %pad_maximum_fusion.1.cs_ref.refs_2_, bf16[4,8,96,768]{3,2,1,0:T(8,128)(2,1)} %bitcast.74, ...), custom_call_target="tpu_custom_call" | custom-call | tf_op jit(solution)/shard_map/middle/pallas_call | solution.py:765
  247.5 0.6 slice_reduce_fusion
  248.1 0.5 copy.55
  248.6 0.2 reduce_sum.108
  248.8 0.2 multiply_reduce_fusion.4
  249.0 1.2 fusion.n1t_ref
  250.2 3.0 copy.59
  253.3 2.4 convert_bitcast_fusion.cb_ref
  255.6 14.4 %returning.1 = (f32[512,768]{1,0:T(8,128)}, f32[512,768]{1,0:T(8,128)}, bf16[4,768,768]{2,1,0:T(8,128)(2,1)}) custom-call(bf16[768,512]{1,0:T(8,128)(2,1)} %fusion.n1t_ref, bf16[768,512]{1,0:T(8,128)(2,1)} %convert_bitcast_fusion.cb_ref, bf16[4,3,512,256]{3,2,1,0:T(8,128)(2,1)} %get-tuple-element.33.z_ref, bf16[4,768,768]{2,1,0:T(8,128)(2,1)} %bitcast.73), custom_call_target="tpu_custom_call" | custom-call | tf_op jit(solution)/shard_map/returning/pallas_call | solution.py:825
  270.0 3.1 copy.60
  273.1 3.0 copy.62
  276.1 3.5 multiply_reduce_fusion
  279.8 1.5 reduce_sum.115
  281.5 1.6 reduce_sum.117
  283.2 1.5 reduce_sum.118
  284.8 0.1 stack.87
  285.5 0.7 fusion.2.refs_2_
  286.2 54.1 %scatter_last.1 = (f32[3,96,768]{2,1,0:T(8,128)}, f32[8,128]{1,0:T(8,128)}) custom-call(bf16[4,8,96,768]{3,2,1,0:T(8,128)(2,1)} %bitcast.72, bf16[2,4,96,768]{3,2,1,0:T(8,128)(2,1)} %get-tuple-element.40.refs_1_, f32[8,4,8,128]{3,2,1,0:T(8,128)} %fusion.2.refs_2_), custom_call_target="tpu_custom_call" | custom-call | tf_op jit(solution)/shard_map/scatter_last/pallas_call | solution.py:917
  340.3 2.1 slice_bitcast_fusion
  342.4 1.1 copy.68
  343.5 0.7 copy.69
  344.2 1.8 copy.71
  346.1 0.6 slice.79
  346.7 1.4 slice_bitcast_fusion.3
  348.1 0.7 slice_reduce_fusion.4
  348.8 0.7 reshape_squeeze.7
  349.5 1.2 slice_bitcast_fusion.4
  350.7 0.7 broadcast_multiply_fusion
  351.3 0.7 broadcast_multiply_fusion.1
  352.0 0.7 broadcast_multiply_fusion.2
  352.7 0.7 broadcast_multiply_fusion.3
  353.4 4.3 %multiply_add_fusion = f32[512,768]{0,1:T(8,128)} fusion(f32[512,768]{0,1:T(8,128)} %copy.59, f32[512,768]{0,1:T(8,128)} %copy.62, f32[512,768]{0,1:T(8,128)} %copy.60, f32[512]{0:T(512)S(1)} %broadcast_multiply_fusion, f32[512]{0:T(512)S(1)} %broadcast_multiply_fusion.1, f32[768]{0:T(1024)S(1)} %get-tuple-element.93, f32[512]{0:T(512)S(1)} %broadcast_multiply_fusion.2, ...), kind=kLoop, calls=%fused_computation.2 | loop fusion | flops 5505024 | bytes 7882752 | tf_op jit(solution)/shard_map/add | solution.py:1013
  357.7 3.1 copy.70
  360.8 2.8 add_add_fusion
  (41 shorter events, 1.1 us)
Async XLA Ops:
  0.6 8.6 %copy-start.3 = (bf16[96,768]{1,0:T(8,128)(2,1)S(1)}, bf16[96,768]{1,0:T(8,128)(2,1)}, u32[]{:S(2)}) copy-start(bf16[96,768]{1,0:T(8,128)(2,1)} %param.25) | copy-start | bytes 442372
  0.7 8.6 %copy-start.2 = (bf16[768,96]{0,1:T(8,128)(2,1)S(1)}, bf16[768,96]{0,1:T(8,128)(2,1)}, u32[]{:S(2)}) copy-start(bf16[768,96]{0,1:T(8,128)(2,1)} %param.27) | copy-start | bytes 442372
  119.5 128.0 %copy-start.7 = (f32[8,768]{1,0:T(8,128)S(1)}, f32[8,768]{1,0:T(8,128)}, u32[]{:S(2)}) copy-start(f32[8,768]{1,0:T(8,128)} %get-tuple-element.29) | copy-start | bytes 73732
  119.5 128.6 %copy-start = (f32[512,768]{1,0:T(8,128)S(1)}, f32[512,768]{1,0:T(8,128)}, u32[]{:S(2)}) copy-start(f32[512,768]{1,0:T(8,128)} %x_ref.1) | copy-start | bytes 4718596
  281.5 3.4 copy-start.4
  281.5 3.8 %copy-start.6 = (f32[4,768]{1,0:T(4,128)S(1)}, f32[4,768]{1,0:T(4,128)}, u32[]{:S(2)}) copy-start(f32[4,768]{1,0:T(4,128)} %get-tuple-element.42) | copy-start | bytes 36868
  357.6 3.1 copy-start.1
  357.7 3.1 copy-start.5

commit v3 on v2

--- a/solution.py
+++ b/solution.py
@@ -40,6 +40,18 @@
     for bit in bits:
         masks = masks + [m | (1 << bit) for m in masks]
     return masks
+
+
+def same(index, value, count):
+    return 1 - ((index + count - value) % count + count - 1) // count
+
+
+def nearest(place, turn, count):
+    out = 0
+    for p in range(count):
+        order = sorted(range(count), key=lambda q: (abs(q - p), q < count - 1 - p))
+        out = out + same(place, p, count) * order[turn]
+    return out
 
 
 def remote(src, dst, send_sem, recv_sem, device):
@@ -117,11 +129,13 @@
     y_ref,
     p_ref,
     small_ref,
-    out_ref,
-    back_ref,
+    two_ref,
+    grad_ref,
     gu_ref,
     gd_ref,
     gb_ref,
+    out_ref,
+    back_ref,
     g_ref,
     x_buf,
     n1_ref,
@@ -152,9 +166,24 @@
     nbits = count.bit_length() - 1
     first = list(range(nbits - 1, -1, -1))
     second = [first[1], first[0]] + first[2:] if nbits >= 3 else first
-    head_chunks = [(0, s, (first, second)[s % 2]) for s in range(places)]
-    feed_chunks = [(a, s, (first, second)[a - 1]) for s in range(places) for a in (1, 2)]
-    chunks = head_chunks + feed_chunks
+    turns = list(range(places))
+    pairs = [
+        tuple((0, t, (first, second)[t % 2]) for t in turns[n : n + 2])
+        for n in range(0, places, 2)
+    ]
+    head_pairs = len(pairs)
+    pairs += [((1, t, first), (2, t, second)) for t in turns]
+    chunks = [chunk for pair in pairs for chunk in pair]
+    numbers, n = [], 0
+    for pair in pairs:
+        numbers.append(list(range(n, n + len(pair))))
+        n += len(pair)
+
+    def source(t):
+        return nearest(mz, t, places)
+
+    def source_at(i):
+        return sum(same(i, t, places) * source(t) for t in turns)
 
     def vec_copy(i, sending):
         di, zi = i // places, i % places
@@ -170,21 +199,33 @@
             ((me + di) % count, (mz + zi) % places),
         )
 
-    def z_copy(a, s, sending):
-        slot = mz if sending else (mz + places - s) % places
-        n = a * (places - 1) + s - 1
+    def z_copy(a, p, up, own=False):
+        src = w_ref.at[a] if own else g_ref.at[a, p, me]
         return remote(
-            w_ref.at[a], g_ref.at[a, slot, me], zs.at[n], zr.at[n], (me, (mz + s) % places)
+            src,
+            g_ref.at[a, p, me],
+            zs.at[(a * places + p) * 2 + (0 if up else 1)],
+            zr.at[a * places + p],
+            (me, mz + 1 if up else mz - 1),
         )
 
+    def pass_on(a, p, own=False):
+        @pl.when((p <= mz) & (mz < places - 1))
+        def _():
+            z_copy(a, p, True, own).start()
+
+        @pl.when((p >= mz) & (mz > 0))
+        def _():
+            z_copy(a, p, False, own).start()
+
     def d_copies(j, k, sending):
-        a, s, order = chunks[j]
-        place = (mz + places - s) % places
+        a, t, order = chunks[j]
+        place = source(t)
         bit = order[k]
         out = []
         for i, m in enumerate(span(order[:k])):
             slot = flip(me, m if sending else m | (1 << bit))
-            src = w_ref.at[a] if s == 0 and m == 0 and sending else g_ref.at[a, place, slot]
+            src = w_ref.at[a] if t == 0 and m == 0 and sending else g_ref.at[a, place, slot]
             n = j * (count - 1) + (1 << k) - 1 + i
             out.append(
                 remote(
@@ -198,10 +239,12 @@
         return out
 
     def step(j, k):
-        a, s, _ = chunks[j]
+        a, t, _ = chunks[j]
         if k == 0:
-            if s > 0:
-                z_copy(a, s, False).wait_recv()
+            if t > 0:
+                p = source(t)
+                z_copy(a, p, True).wait_recv()
+                pass_on(a, p)
         else:
             for copy in d_copies(j, k - 1, False):
                 copy.wait_recv()
@@ -209,21 +252,37 @@
             for copy in d_copies(j, k, True):
                 copy.start()
 
-    def slot_steps(slot, low, high, lag, skip=()):
-        for k in range(nbits, -1, -1):
-            pair = slot - lag * k
-            for j in (low + 2 * pair, low + 2 * pair + 1):
-                if pair >= 0 and j < high and (j, k) not in skip:
-                    step(j, k)
-
-    def x_copy(h, s, sending):
-        to = (mz + s) % places
-        slot = mz if sending else (mz + places - s) % places
-        n = h * places + s
-        return remote(x_buf.at[to, h], y_ref.at[h, slot], xs.at[n], xr.at[n], (me, to))
+    def pair_step(pair, k):
+        for j in numbers[pair]:
+            if k > 0 or chunks[j][1] > 0:
+                step(j, k)
+
+    def x_copy(h, p, sending):
+        slot = mz if sending else p
+        return remote(
+            x_buf.at[p, h],
+            y_ref.at[h, slot],
+            xs.at[h * places + p],
+            xr.at[h * places + slot],
+            (me, p),
+        )
 
     def keep_own(h):
         return pltpu.make_async_copy(x_buf.at[mz, h], y_ref.at[h, mz], ls.at[5 + h])
+
+    schedule = []
+    for pair in range(len(pairs)):
+        head = pair < head_pairs
+        for k in range(nbits + 1):
+            at = 3 * k + 2 * pair if head else 3 * k + 2 * pair + 2
+            schedule.append((at, -k, pair))
+    schedule = [(pair, -k) for _, k, pair in sorted(schedule)]
+    head_done = max(i for i, (p, k) in enumerate(schedule) if p < head_pairs and k == nbits) + 1
+    feed_done = [schedule.index((head_pairs + t, nbits)) + 1 for t in turns]
+
+    def run(low, high):
+        for pair, k in schedule[low:high]:
+            pair_step(pair, k)
 
     own = [
         pltpu.make_async_copy(w_ref.at[a], g_ref.at[a, mz, me], ls.at[a]) for a in range(3)
@@ -236,20 +295,18 @@
 
     lax.fori_loop(1, total, send_vec, 0)
     own_vec.start()
-    heads_end = len(head_chunks)
-    end = len(chunks)
-    early = [(0, 0), (heads_end, 0), (heads_end + 1, 0)]
-    for j, k in early:
-        step(j, k)
+    for j in [n for n, chunk in enumerate(chunks) if chunk[1] == 0]:
+        step(j, 0)
     for a in range(3):
-        for s in range(1, places):
-            z_copy(a, s, True).start()
+        pass_on(a, mz, True)
     for copy in own:
         copy.start()
 
     mine = cs_ref[:, pl.ds(pl.multiple_of(mz * rows, rows), rows)]
     for i, table in enumerate(spread_turns(mine)):
         table_ref[i] = table
+
+    run(0, 2)
 
     def wait_vec(i, carry):
         vec_copy(i, False).wait_recv()
@@ -307,28 +364,27 @@
         cb_ref[here, :] = cot.astype(BF)
         cbt_ref[:, here] = cot.T.astype(BF)
 
-    slot_count = (heads_end + 1) // 2 + nbits
-    for slot in range(slot_count):
-        slot_steps(slot, 0, heads_end, 1, early)
-        if slot < 4:
-            norm(slot)
-    for i in range(slot_count, 4):
-        norm(i)
+    cuts = [2 + (head_done - 2) * i // 5 for i in range(6)]
+    for i in range(5):
+        run(cuts[i], cuts[i + 1])
+        if i < 4:
+            norm(i)
     own[0].wait()
     save = pltpu.make_async_copy(g_ref.at[0], p_ref, ls.at[4])
     save.start()
 
-    lag = 2
     heads = ff // GROUP
+    before_feed = max(feed_done[0], head_done)
+    cuts = [head_done + (before_feed - head_done) * i // places for i in range(places + 1)]
 
     def project(i, carry):
-        for slot in range(places):
-
-            @pl.when(i == slot)
-            def _():
-                slot_steps(slot, heads_end, end, lag, early)
-
-        to = (mz + 1 + i) % places
+        for n in range(places):
+
+            @pl.when(i == n)
+            def _(n=n):
+                run(cuts[n], cuts[n + 1])
+
+        to = source_at((i + 1) % places)
         w = g_ref[0, to].reshape(model, ff)
         forward = dot(n1_ref[...], w, 1, 0) + bq_ref[pl.ds(to, 1), :]
         column = lax.broadcasted_iota(jnp.int32, (rows, LANES), 1)
@@ -344,7 +400,7 @@
         @pl.when(i < places - 1)
         def _():
             for h in range(heads):
-                x_copy(h, 1 + i, True).start()
+                x_copy(h, to, True).start()
 
         @pl.when(i == places - 1)
         def _():
@@ -362,7 +418,7 @@
     width = ff // 2
 
     def puts(i):
-        place = (mz + places - i) % places
+        place = source_at(i)
         return [
             pltpu.make_async_copy(
                 buf.at[i], ref.at[place], ls.at[5 + heads + 2 * i + a]
@@ -371,18 +427,17 @@
         ]
 
     def feed(f, carry):
-        slot = places
-        for i in range(places):
-            until = i + lag * nbits
-
-            @pl.when(f == 2 * i)
-            def _(slot=slot, until=until):
-                for t in range(slot, until + 1):
-                    slot_steps(t, heads_end, end, lag, early)
-
-            slot = max(slot, until + 1)
+        low = before_feed
+        for t in turns:
+            high = max(low, feed_done[t])
+
+            @pl.when(f == 2 * t)
+            def _(low=low, high=high):
+                run(low, high)
+
+            low = high
         i, h = f // 2, f % 2
-        place = (mz + places - i) % places
+        place = source_at(i)
         cols = pl.ds(pl.multiple_of(h * width, width), width)
         up = g_ref[1, place, :, :, cols].reshape(model, width)
         down = g_ref[2, place, :, :, cols].reshape(model, width)
@@ -407,16 +462,26 @@
 
     lax.fori_loop(0, 2 * places, feed, 0)
 
-    save.wait()
+    saves = [
+        pltpu.make_async_copy(buf, ref, ls.at[5 + heads + 2 * places + i])
+        for i, (buf, ref) in enumerate(((out_ref, two_ref), (back_ref, grad_ref)))
+    ]
+    for copy in saves:
+        copy.start()
+    for copy in [save] + saves:
+        copy.wait()
     for i in range(places):
         for copy in puts(i):
             copy.wait()
     for h in range(heads):
         keep_own(h).wait()
-        for s in range(1, places):
-            x_copy(h, s, False).wait_recv()
-        for s in range(1, places):
-            x_copy(h, s, True).wait_send()
+        for p in range(places):
+
+            @pl.when(p != mz)
+            def _(h=h, p=p):
+                x_copy(h, p, False).wait_recv()
+                x_copy(h, p, True).wait_send()
+
 
     def wait_sent(i, carry):
         vec_copy(i, True).wait_send()
@@ -424,8 +489,16 @@
 
     lax.fori_loop(1, total, wait_sent, 0)
     for a in range(3):
-        for s in range(1, places):
-            z_copy(a, s, True).wait_send()
+        for p in range(places):
+
+            @pl.when((p <= mz) & (mz < places - 1))
+            def _(a=a, p=p):
+                z_copy(a, p, True).wait_send()
+
+            @pl.when((p >= mz) & (mz > 0))
+            def _(a=a, p=p):
+                z_copy(a, p, False).wait_send()
+
     for j in range(len(chunks)):
         for k in range(nbits):
             for copy in d_copies(j, k, True):
@@ -452,8 +525,10 @@
             shape((places, ff), F32),
         ),
         in_specs=[VMEM] * 5,
-        out_specs=(ANY, ANY, VMEM, VMEM, VMEM, ANY, ANY, VMEM),
+        out_specs=(ANY, ANY, VMEM, ANY, ANY, ANY, ANY, VMEM),
         scratch_shapes=[
+            pltpu.VMEM((rows, model), F32),
+            pltpu.VMEM((rows, model), F32),
             pltpu.VMEM((3, places, count, depth, ff), BF),
             pltpu.VMEM((places, heads, rows, GROUP), BF),
             pltpu.VMEM((rows, model), BF),
@@ -467,15 +542,15 @@
             pltpu.VMEM((places, ff), F32),
             pltpu.VMEM((places, model, ff), BF),
             pltpu.VMEM((places, model, ff), BF),
-            sem((3 * (places - 1),)),
-            sem((3 * (places - 1),)),
+            sem((6 * places,)),
+            sem((3 * places,)),
             sem((3 * places * (count - 1),)),
             sem((3 * places * (count - 1),)),
             sem((total,)),
             sem((total,)),
             sem((heads * places,)),
             sem((heads * places,)),
-            sem((5 + heads + 2 * places,)),
+            sem((7 + heads + 2 * places,)),
         ],
         compiler_params=pltpu.CompilerParams(
             has_side_effects=True, vmem_limit_bytes=VMEM_LIMIT
@@ -596,7 +671,6 @@
     rows = total // places
     scale = HD**-0.5
     nq = total // wq
-    ratio = wq // wk
 
     chunks = []
     for s in list(range(1, places)) + [0]:
@@ -610,7 +684,7 @@
     for k in range(nbits):
         for pair in range(len(chunks) // 2):
             when = (2 + pair // 2, 5 + pair)[k] if k < 2 else 9 + pair + 4 * (k - 2)
-            events.setdefault(min(when, last_step), []).append((pair, k))
+            events.setdefault(min(when * nq // 4, last_step), []).append((pair, k))
 
     def run_events(step):
         for pair, k in events.get(step, []):
@@ -674,7 +748,7 @@
         begin = begin_ref[0:1, at]
         last = i * wq + lax.broadcasted_iota(jnp.int32, (1, wq), 1)
         query, grad = qh[at, :], oh[at, :]
-        trips = (i + 1) * ratio
+        trips = ((i + 1) * wq + wk - 1) // wk
 
         def scores(j, peak):
             keys = pl.ds(pl.multiple_of(j * wk, wk), wk)
@@ -758,7 +832,7 @@
 def middle(y, begin, turns, up_grad, down_grad):
     heads, total, group = y.shape
     places, count, depth, ff = up_grad.shape
-    wq, wk = min(512, total), min(256, total)
+    wq, wk = min(512, total), min(512, total)
     vmem = pltpu.VMEM
     sem = pltpu.SemaphoreType.DMA
     shape = jax.ShapeDtypeStruct
@@ -786,100 +860,91 @@
     )(y, begin, turns, up_grad, down_grad)
 
 
-def return_kernel(n1t_ref, cb_ref, z_ref, w_ref, out_ref, back_ref, g_ref):
-    @pl.when(pl.program_id(0) == 0)
-    def _():
-        out_ref[...] = jnp.zeros_like(out_ref)
-        back_ref[...] = jnp.zeros_like(back_ref)
-
-    heads = z_ref.shape[1]
-    rows = z_ref.shape[2]
-    model = w_ref.shape[1]
-    left = lax.broadcasted_iota(jnp.int32, (rows, LANES), 1) < HD
-    wide_left = lax.broadcasted_iota(jnp.int32, (model, LANES), 1) < HD
-    out, back = out_ref[...], back_ref[...]
-    for h in range(heads):
-        z = z_ref[0, h]
-        w = w_ref[0, :, h * GROUP : (h + 1) * GROUP]
-        late = z[:, LANES:]
-        none = jnp.zeros_like(late)
-        ours = jnp.concatenate([z[:, :LANES], jnp.where(left, late, none)], axis=1)
-        back = back + dot(ours, w, 1, 1)
-        out = out + dot(jnp.where(left, none, late), w[:, LANES:], 1, 1)
-        first = dot(n1t_ref[...], z, 1, 0)
-        second = dot(cb_ref[...], late, 1, 0)
-        g_ref[0, :, h * GROUP : h * GROUP + LANES] = first[:, :LANES].astype(BF)
-        g_ref[0, :, h * GROUP + LANES : (h + 1) * GROUP] = jnp.where(
-            wide_left, first[:, LANES:], second
-        ).astype(BF)
-    out_ref[...] = out
-    back_ref[...] = back
-
-
-def returning(n1, cot, z, w):
-    places, heads, rows, group = z.shape
-    model, width = w.shape[1:]
-    turned = pl.BlockSpec((model, rows), lambda z: (0, 0))
-    whole = pl.BlockSpec((rows, model), lambda z: (0, 0))
-    square = pl.BlockSpec((1, model, width), lambda z: (z, 0, 0))
-    return pl.pallas_call(
-        return_kernel,
-        grid=(places,),
-        out_shape=(
-            jax.ShapeDtypeStruct((rows, model), F32),
-            jax.ShapeDtypeStruct((rows, model), F32),
-            jax.ShapeDtypeStruct((places, model, width), BF),
-        ),
-        in_specs=[
-            turned,
-            turned,
-            pl.BlockSpec((1, heads, rows, group), lambda z: (z, 0, 0, 0)),
-            square,
-        ],
-        out_specs=(whole, whole, square),
-        compiler_params=pltpu.CompilerParams(vmem_limit_bytes=VMEM_LIMIT),
-        name="returning",
-    )(n1.T, cot.T, z, w)
-
-
-def last_kernel(count, places, *refs):
-    g_ref, red_ref, vec_ref, out_ref, vout_ref, zb, vb, zs, zr, vs, vr, ls, acc = refs[:13]
+def place_rows(values, pick, keep):
+    return lax.dot_general(
+        jnp.where(keep, values, 0.0),
+        pick,
+        (((1,), (0,)), ((), ())),
+        precision=lax.Precision.HIGHEST,
+        preferred_element_type=F32,
+    )
+
+
+def tail_kernel(count, places, wide, piece, *refs):
+    x_hbm, cot_hbm, z_hbm, w_hbm, two_hbm, grad_hbm, small_ref, red_ref, qb_ref, gb_ref = refs[:10]
+    y_ref, dx_ref, gq_ref, gp_ref, gu_ref, gd_ref, vout_ref = refs[10:17]
+    x_ref, cot_ref, z_ref, w_ref, two_ref, grad_ref = refs[17:23]
+    normal_ref, inverse_ref, n1t_ref, cbt_ref, out_ref, back_ref, g_ref = refs[23:30]
+    sums_ref, vec_ref, zb, vb, zs, zr, vs, vr, ls, acc = refs[30:40]
     nbits = count.bit_length() - 1
-    landing = refs[13 : 13 + nbits]
-    send, recv, local = refs[13 + nbits :]
+    landing = refs[40 : 40 + nbits]
+    send, recv, local = refs[40 + nbits :]
     me, mz = lax.axis_index("dp"), lax.axis_index("tensor")
     total = count * places
+    rows, model = x_ref.shape
+    heads = z_ref.shape[1]
+    depth, ff = acc.shape[2:]
+
+    chunks = [
+        (0, s, Scatter.orders(count)[i % 2])
+        for i, s in enumerate(list(range(1, places)) + [0])
+    ]
+    scatter = Scatter(count, places, chunks, (g_ref,), acc, landing, (send, recv), local)
+
+    def z_copy(a, s):
+        n = a * (places - 1) + s - 1
+        src = acc.at[s - 1, 0] if a == 0 else red_ref.at[a - 1, s]
+        return remote(src, zb.at[a, s - 1], zs.at[n], zr.at[n], (me, (mz + s) % places))
 
     def vec_copy(i, sending):
         to = ((me + i // places) % count, (mz + i % places) % places)
-        return remote(vec_ref.at[to[0], to[1]], vb.at[i], vs.at[i], vr.at[i], to)
-
-    def send_vec(i, carry):
-        vec_copy(i, True).start()
-        return carry
-
-    chunks = []
-    for i, s in enumerate(list(range(1, places)) + [0]):
-        chunks.append((0, s, Scatter.orders(count)[i % 2]))
-    scatter = Scatter(count, places, chunks, (g_ref,), acc, landing, (send, recv), local)
-    for j in range(len(chunks)):
-        scatter.start(j)
-
-    def z_copy(a, s):
-        n = a * (places - 1) + s - 1
-        if a == 0:
-            src = acc.at[s - 1, 0]
-        else:
-            src = red_ref.at[a - 1, s]
-        return remote(src, zb.at[a, s - 1], zs.at[n], zr.at[n], (me, (mz + s) % places))
-
-    for a in (1, 2):
-        for s in range(1, places):
+        return remote(
+            vec_ref.at[to[0] * places + to[1]], vb.at[i], vs.at[i], vr.at[i], to
+        )
+
+    def fetch(i):
+        at = (mz + 1 + i) % places
+        return [
+            pltpu.make_async_copy(z_hbm.at[at], z_ref.at[at], ls.at[4 + 2 * i]),
+            pltpu.make_async_copy(w_hbm.at[at], w_ref.at[at], ls.at[5 + 2 * i]),
+        ]
+
+    inputs = [
+        pltpu.make_async_copy(src, dst, ls.at[i])
+        for i, (src, dst) in enumerate(
+            ((x_hbm, x_ref), (cot_hbm, cot_ref), (two_hbm, two_ref), (grad_hbm, grad_ref))
+        )
+    ]
+    for copy in inputs[:2]:
+        copy.start()
+    for i in range(places):
+        for copy in fetch(i):
+            copy.start()
+    for copy in inputs[2:]:
+        copy.start()
+    for s in range(1, places):
+        for a in (1, 2):
             z_copy(a, s).start()
-    lax.fori_loop(1, total, send_vec, 0)
-    own_vec = pltpu.make_async_copy(vec_ref.at[me, mz], vb.at[0], ls.at[0])
-    own_vec.start()
-    for slot in range((len(chunks) + 1) // 2 + nbits - 1):
+
+    blocks = 4
+    block = rows // blocks
+    for copy in inputs[:2]:
+        copy.wait()
+    for i in range(blocks):
+        here = slice(i * block, (i + 1) * block)
+        values = x_ref[here, :]
+        center = values - jnp.mean(values, axis=1, keepdims=True)
+        inverse = lax.rsqrt(jnp.mean(center * center, axis=1, keepdims=True) + EPSILON)
+        normal = center * inverse
+        normal_ref[here, :] = normal
+        inverse_ref[here, :] = jnp.broadcast_to(inverse, (block, LANES))
+        mixed = normal * small_ref[0:1, :] + small_ref[1:2, :]
+        n1t_ref[:, here] = mixed.T.astype(BF)
+        cbt_ref[:, here] = cot_ref[here, :].T.astype(BF)
+    out_ref[...] = jnp.zeros_like(out_ref)
+    back_ref[...] = jnp.zeros_like(back_ref)
+
+    def steps(slot):
         for k in range(nbits - 1, -1, -1):
             pair = slot - k
             for j in (2 * pair, 2 * pair + 1):
@@ -887,6 +952,132 @@
                     scatter.stage(j, k)
                     if k == nbits - 1 and chunks[j][1] > 0:
                         z_copy(0, chunks[j][1]).start()
+
+    left = lax.broadcasted_iota(jnp.int32, (rows, LANES), 1) < HD
+    wide_left = lax.broadcasted_iota(jnp.int32, (model, LANES), 1) < HD
+
+    def source(i, carry):
+        at = (mz + 1 + i) % places
+        for n in range(places):
+
+            @pl.when(i == n)
+            def _():
+                for copy in fetch(n):
+                    copy.wait()
+
+        def head(h, carry):
+            z = z_ref[at, h]
+            start = pl.multiple_of(h * GROUP, GROUP)
+            w = w_ref[at, :, :, pl.ds(start, GROUP)].reshape(model, GROUP)
+            late = z[:, LANES:]
+            none = jnp.zeros_like(late)
+            ours = jnp.concatenate([z[:, :LANES], jnp.where(left, late, none)], axis=1)
+            back_ref[...] += dot(ours, w, 1, 1)
+            out_ref[...] += dot(jnp.where(left, none, late), w[:, LANES:], 1, 1)
+            first = dot(n1t_ref[...], z, 1, 0)
+            second = dot(cbt_ref[...], late, 1, 0)
+            g_ref[at, :, :, pl.ds(start, LANES)] = (
+                first[:, :LANES].astype(BF).reshape(count, depth, LANES)
+            )
+            second = jnp.where(wide_left, first[:, LANES:], second)
+            g_ref[at, :, :, pl.ds(start + LANES, LANES)] = second.astype(BF).reshape(
+                count, depth, LANES
+            )
+            return carry
+
+        lax.fori_loop(0, heads, head, 0)
+        for n in range(places):
+
+            @pl.when(i == n)
+            def _():
+                scatter.start(n)
+                if n % 2 == 0 and n > 0:
+                    steps(n // 2 - 1)
+
+        return carry
+
+    lax.fori_loop(0, places, source, 0)
+    slot = max((places - 1) // 2, 0)
+    last = (len(chunks) + 1) // 2 + nbits - 1
+
+    for copy in inputs[2:]:
+        copy.wait()
+    sums = [jnp.zeros((8, model), F32) for _ in range(5)]
+
+    def norm_rows_back(grad, gain, normal, inverse):
+        scaled = grad * gain
+        first = jnp.mean(scaled, axis=1, keepdims=True)
+        second = jnp.mean(scaled * normal, axis=1, keepdims=True)
+        return inverse * (scaled - first - normal * second)
+
+    def fold(values):
+        return jnp.sum(values.reshape(block // 8, 8, model), axis=0)
+
+    for i in range(blocks):
+        here = slice(i * block, (i + 1) * block)
+        normal, inverse = normal_ref[here, :], inverse_ref[here, 0:1]
+        cot, one, two = cot_ref[here, :], back_ref[here, :], grad_ref[here, :]
+        y_ref[here, :] = (
+            x_ref[here, :] + (out_ref[here, :] + two_ref[here, :]) + small_ref[4:5, :]
+        )
+        dx_ref[here, :] = (
+            cot
+            + norm_rows_back(one, small_ref[0:1, :], normal, inverse)
+            + norm_rows_back(two, small_ref[2:3, :], normal, inverse)
+        )
+        for r, values in enumerate((one * normal, one, two * normal, two, cot)):
+            sums[r] = sums[r] + fold(values)
+        if slot < last:
+            steps(slot)
+            slot += 1
+    sums_ref[...] = jnp.zeros_like(sums_ref)
+    for r in range(5):
+        sums_ref[r : r + 1, :] = jnp.sum(sums[r], axis=0, keepdims=True)
+
+    lane = lax.broadcasted_iota(jnp.int32, (1, ff), 1)
+    line = lax.broadcasted_iota(jnp.int32, (ff, 1), 0)
+    out_lane = lax.broadcasted_iota(jnp.int32, (1, LANES), 1)
+    sub = lax.broadcasted_iota(jnp.int32, (total * 8, 1), 0)
+    who, what = sub // 8, sub % 8
+    spread = jnp.broadcast_to(sums_ref[...][None], (total, 8, model)).reshape(total * 8, model)
+    parts = place_rows(
+        spread,
+        jnp.where(line % piece == out_lane, 1.0, 0.0),
+        (what < 5) & (who == lane // piece),
+    )
+    each = wide // count
+    kind, inner = lane % GROUP // HD, lane // GROUP * HD + lane % HD
+    kind_line, inner_line = line % GROUP // HD, line // GROUP * HD + line % HD
+    qkv = jnp.concatenate(
+        [jnp.sum(qb_ref[h], axis=0, keepdims=True) for h in range(heads)], axis=1
+    )
+    parts += place_rows(
+        jnp.broadcast_to(qkv, (total * 8, ff)),
+        jnp.where(kind_line * each + inner_line % each == out_lane, 1.0, 0.0),
+        (what == 5) & (kind < 3) & (who == inner // each * places + mz),
+    )
+    each = ff // count
+    up = jnp.zeros((total * 8, ff), F32)
+    for z in range(places):
+        up = jnp.where(who % places == z, gb_ref[z : z + 1, :], up)
+    parts += place_rows(
+        up,
+        jnp.where(line % each == out_lane, 1.0, 0.0),
+        (what == 6) & (who // places == lane // each),
+    )
+    vec_ref[...] = parts.reshape(total, 8, LANES)
+
+    def send_vec(i, carry):
+        vec_copy(i, True).start()
+        return carry
+
+    lax.fori_loop(1, total, send_vec, 0)
+    own_vec = pltpu.make_async_copy(vec_ref.at[me * places + mz], vb.at[0], ls.at[4 + 2 * places])
+    own_vec.start()
+    while slot < last:
+        steps(slot)
+        slot += 1
+
     own_vec.wait()
 
     def wait_vec(i, carry):
@@ -903,49 +1094,76 @@
         result = own.astype(F32)
         for s in range(1, places):
             result = result + zb[a, s - 1].astype(F32)
-        out_ref[a] = result
+        if a == 1:
+            gu_ref[...] = result
+        elif a == 2:
+            gd_ref[...] = result.T
+        else:
+            for h in range(heads):
+                for c, ref in enumerate((gq_ref.at[0], gq_ref.at[1], gq_ref.at[2])):
+                    ref[:, h * HD : (h + 1) * HD] = result[
+                        :, h * GROUP + c * HD : h * GROUP + (c + 1) * HD
+                    ]
+                gp_ref[h * HD : (h + 1) * HD, :] = result[
+                    :, h * GROUP + 3 * HD : (h + 1) * GROUP
+                ].T
     scatter.drain()
     for a in range(3):
         for s in range(1, places):
             z_copy(a, s).wait_send()
 
 
-def scatter_last(grad, partly, vectors):
-    places, count, rows, width = grad.shape
+def tail(x, cot, z, w, two, grad, small, partly, qkv_sums, up_sums, wide, piece):
+    places, heads, rows, group = z.shape
+    count, depth, ff = w.shape[1:]
+    model = x.shape[1]
     total = count * places
     sem = pltpu.SemaphoreType.DMA
+    shape = jax.ShapeDtypeStruct
+    vmem = pltpu.VMEM
     return pl.pallas_call(
-        functools.partial(last_kernel, count, places),
+        functools.partial(tail_kernel, count, places, wide, piece),
         out_shape=(
-            jax.ShapeDtypeStruct((3, rows, width), F32),
-            jax.ShapeDtypeStruct(vectors.shape[2:], F32),
+            shape((rows, model), F32),
+            shape((rows, model), F32),
+            shape((3, depth, wide), F32),
+            shape((wide, depth), F32),
+            shape((depth, ff), F32),
+            shape((ff, depth), F32),
+            shape((8, LANES), F32),
         ),
-        in_specs=[ANY, VMEM, ANY],
-        out_specs=(VMEM, VMEM),
+        in_specs=[ANY] * 6 + [VMEM] * 4,
+        out_specs=(VMEM,) * 7,
         scratch_shapes=[
-            pltpu.VMEM((3, places - 1, rows, width), BF),
-            pltpu.VMEM((total,) + vectors.shape[2:], F32),
+            vmem((rows, model), F32),
+            vmem((rows, model), F32),
+            vmem((places, heads, rows, group), BF),
+            vmem((places, count, depth, ff), BF),
+            vmem((rows, model), F32),
+            vmem((rows, model), F32),
+            vmem((rows, model), F32),
+            vmem((rows, LANES), F32),
+            vmem((model, rows), BF),
+            vmem((model, rows), BF),
+            vmem((rows, model), F32),
+            vmem((rows, model), F32),
+            vmem((places, count, depth, ff), BF),
+            vmem((8, model), F32),
+            vmem((total, 8, LANES), F32),
+            vmem((3, places - 1, depth, ff), BF),
+            vmem((total, 8, LANES), F32),
             sem((3 * (places - 1),)),
             sem((3 * (places - 1),)),
             sem((total,)),
             sem((total,)),
-            sem((1,)),
+            sem((5 + 2 * places,)),
         ]
-        + Scatter.scratch(count, places, rows, width),
+        + Scatter.scratch(count, places, depth, ff),
         compiler_params=pltpu.CompilerParams(
             has_side_effects=True, vmem_limit_bytes=VMEM_LIMIT
         ),
-        name="scatter_last",
-    )(grad, partly, vectors)
-
-
-def norm_back(grad_out, normal, inverse, gain):
-    scaled = grad_out * gain
-    return inverse * (
-        scaled
-        - jnp.mean(scaled, axis=1, keepdims=True)
-        - normal * jnp.mean(scaled * normal, axis=1, keepdims=True)
-    )
+        name="tail",
+    )(x, cot, z, w, two, grad, small, partly, qkv_sums, up_sums)
 
 
 def lanes(values, width=LANES):
@@ -978,7 +1196,6 @@
     ff = up_weight.shape[1]
     piece = first_gain.shape[0]
     total = segment_ids.shape[0]
-    place = lax.axis_index("tensor")
 
     attn = jnp.stack([qkv_weight[0], qkv_weight[1], qkv_weight[2], proj_weight.T])
     attn = attn.reshape(4, depth, heads, HD).transpose(1, 2, 0, 3).reshape(depth, 4 * wide)
@@ -993,8 +1210,6 @@
     y, attn_weights, small, out_two, grad_two, up_grad, down_grad, up_bias_part = front(
         block_input, cotangent, packed, vector, turns, count, places, wide, piece
     )
-    attn_weights = attn_weights.reshape(places, model, ff)
-    gain_one, shift_one, gain_two, shift_two, bias_out = (small[i] for i in range(5))
     z, qkv_bias_part, partly = middle(
         y.reshape(heads, total, GROUP),
         begin,
@@ -1002,38 +1217,20 @@
         up_grad.reshape(places, count, depth, ff),
         down_grad.reshape(places, count, depth, ff),
     )
-    center = block_input - jnp.mean(block_input, axis=1, keepdims=True)
-    inverse = lax.rsqrt(jnp.mean(center * center, axis=1, keepdims=True) + EPSILON)
-    normal = center * inverse
-    n1 = (normal * gain_one + shift_one).astype(BF)
-    out_one, grad_one, attn_grad = returning(n1, cotangent.astype(BF), z, attn_weights)
-
-    block_output = block_input + (out_one + out_two) + bias_out
-    input_grad = (
-        cotangent
-        + norm_back(grad_one, normal, inverse, gain_one)
-        + norm_back(grad_two, normal, inverse, gain_two)
-    )
-    sums = jnp.stack(
-        [
-            jnp.sum(grad_one * normal, axis=0),
-            jnp.sum(grad_one, axis=0),
-            jnp.sum(grad_two * normal, axis=0),
-            jnp.sum(grad_two, axis=0),
-            jnp.sum(cotangent, axis=0),
-        ]
-    )
-    sums = lanes(sums.reshape(5, count, places, piece).transpose(1, 2, 0, 3))
-    qkv_sum = jnp.sum(qkv_bias_part, axis=1).reshape(heads, 4, HD)[:, :3].transpose(1, 0, 2)
-    qkv_sum = qkv_sum.reshape(3, count, wide // count).transpose(1, 0, 2)
-    qkv_sum = lanes(qkv_sum.reshape(count, 1, 3 * wide // count))
-    here = jnp.arange(places, dtype=jnp.int32)[None, :, None, None] == place
-    qkv_sum = jnp.where(here, qkv_sum[:, None], 0.0)
-    up_sum = lanes(up_bias_part.reshape(places, count, ff // count).transpose(1, 0, 2))[:, :, None]
-    parts = jnp.concatenate([sums, qkv_sum, up_sum, jnp.zeros_like(up_sum)], axis=2)
-
-    done, vec = scatter_last(attn_grad.reshape(places, count, depth, ff), partly, parts)
-    attn_done = done[0].reshape(depth, heads, 4, HD).transpose(2, 0, 1, 3).reshape(4, depth, wide)
+    block_output, input_grad, gq, gp, gu, gd, vec = tail(
+        block_input,
+        cotangent,
+        z,
+        attn_weights,
+        out_two,
+        grad_two,
+        small,
+        partly,
+        qkv_bias_part,
+        up_bias_part,
+        wide,
+        piece,
+    )
     return (
         block_output,
         input_grad,
@@ -1041,12 +1238,12 @@
         vec[1, :piece],
         vec[2, :piece],
         vec[3, :piece],
-        attn_done[:3],
+        gq,
         vec[5, : 3 * wide // count].reshape(3, wide // count),
-        attn_done[3].T,
-        done[1],
+        gp,
+        gu,
         vec[6, : ff // count],
-        done[2].T,
+        gd,
         vec[4, :piece],
     )
 

time: 365 us -> 309 us (0.85)
  other arithmetic: 27.5 us -> 4.69 us
  Pallas kernels: 306 us -> 286 us
  local copies, waits for them, and re-layouts: 29.3 us -> 16.4 us
    pallas_call x1, Pallas kernels: 128 us -> 97.2 us  [middle(): pl.pallas_call(functools.partial(middle_kernel, count, places, heads, wq,...]
    pallas_call x1, Pallas kernels: 109 us -> 126 us  [front(): pl.pallas_call(functools.partial(front_kernel, count, places, wide, piece...]
    reduce_sum x7 -> x0, other arithmetic: 8.57 us -> none  [the longest x1 3.53 us: shards(): jnp.sum(grad_two * normal, axis=0)]
    add x2 -> x0, other arithmetic: 7.14 us -> none  [the longest x1 4.3 us: shards(): cotangent + norm_back(grad_one, normal, inverse, gain_one)]
    pallas_call x2 -> x0, local copies, waits for them, and re-layouts: 6.07 us -> none  [the longest x1 3.05 us: returning(): pl.pallas_call(return_kernel, grid=(places,), out_shape=(jax.ShapeDtypeSt...]
    pallas_call x2 -> x1, Pallas kernels: 68.5 us -> 63.6 us  [tail(): pl.pallas_call(functools.partial(tail_kernel, count, places, wide, piece)...]
    unnamed x21 -> x19, local copies, waits for them, and re-layouts: 9.56 us -> 8.94 us
where the time goes in v3:
time: 309 us; the launch traced here: 308 us
  Pallas kernels  286 us (93%)
  local copies, waits for them, and re-layouts  16.4 us (5%)
  other arithmetic  4.69 us (2%)
    pallas_call x1, Pallas kernels, front(): pl.pallas_call(functools.partial(front_kernel, count, places, wide, piece...  126 us
    pallas_call x1, Pallas kernels, middle(): pl.pallas_call(functools.partial(middle_kernel, count, places, heads, wq,...  97.2 us
    pallas_call x1, Pallas kernels, tail(): pl.pallas_call(functools.partial(tail_kernel, count, places, wide, piece)...  63.6 us
    unnamed x19, local copies, waits for them, and re-layouts  8.94 us

profile of v3, /device:TPU:0, one launch (start us, length us, event | category | flops | bytes accessed | tf_op | source)
XLA Modules:
  0.0 308.2 jit_solution(5017292717869837600)
XLA Ops:
  0.6 0.0 copy-start.3
  0.7 0.0 copy-start.4
  0.7 0.7 pad_bitcast_fusion.4
  1.4 0.8 reshape.51
  2.1 0.7 bitcast_convert_fusion
  2.8 0.7 pad_bitcast_fusion.2
  3.5 0.7 pad_bitcast_fusion
  4.2 0.6 stack.63.vec_ref
  4.8 1.4 iota_subtract_fusion
  6.1 0.3 multiply_cosine_fusion
  6.5 0.7 pad_maximum_fusion.1.cs_ref.refs_2_
  7.1 1.1 copy.30
  8.2 0.8 maximum_bitcast_fusion
  9.1 0.1 copy.32
  9.2 0.0 copy-done.3
  9.2 0.0 copy-done.4
  9.2 0.8 pad_maximum_fusion.w_ref
  10.0 125.5 %front.1 = (bf16[3,4,512,256]{3,2,1,0:T(8,128)(2,1)}, bf16[4,8,96,768]{3,2,1,0:T(8,128)(2,1)}, f32[8,768]{1,0:T(8,128)}, f32[512,768]{1,0:T(8,128)}, f32[512,768...) custom-call(f32[512,768]{1,0:T(8,128)} %refs_0_.1, ...), custom_call_target="tpu_custom_call" | custom-call | tf_op jit(solution)/shard_map/front/pallas_call | solution.py:515
  135.6 97.2 %middle.1 = (bf16[4,3,512,256]{3,2,1,0:T(8,128)(2,1)}, f32[3,8,256]{2,1,0:T(8,128)}, bf16[2,4,96,768]{3,2,1,0:T(8,128)(2,1)}) custom-call(bf16[3,2048,256]{2,1,0:T(8,128)(2,1)} %bitcast.45, s32[1,2048]{1,0:T(1,128)} %bitcast.51, f32[16,2048]{1,0:T(8,128)} %pad_maximum_fusion.1.cs_ref.refs_2_, bf16[4,8,96,768]{3,2,1,0:T(8,128)(2,1)} %bitcast.43, ...), custom_call_target="tpu_custom_call" | custom-call | tf_op jit(solution)/shard_map/middle/pallas_call | solution.py:839
  232.8 63.6 %tail.1 = (f32[512,768]{1,0:T(8,128)}, f32[512,768]{1,0:T(8,128)}, f32[3,96,192]{2,1,0:T(8,128)}, f32[192,96]{1,0:T(8,128)}, f32[96,768]{1,0:T(8,128)}, /*index=5*/f32[768,96]{1,0:T(8,128)}, f32[8,128]{1,0:T(8,128)}) custom-call(f32[512,768]{1,0:T(8,128)} %refs_0_.1, f32[512,768]{1,0:T(8,128)} %refs_1_.1, ...), custom_call_target="tpu_custom_call" | custom-call | tf_op jit(solution)/shard_map/tail/pallas_call | solution.py:1124
  296.4 1.2 slice_bitcast_fusion.1
  297.6 0.7 slice_reduce_fusion
  298.2 1.4 slice_bitcast_fusion
  299.6 0.7 reshape_squeeze.3
  300.3 1.9 copy.33
  302.2 0.0 copy-start
  302.2 2.8 copy.39
  304.9 0.0 copy-done
  304.9 0.0 copy-start.2
  304.9 0.0 copy-start.5
  304.9 0.0 copy-start.1
  304.9 1.1 copy.40
  306.1 0.0 copy-done.2
  306.1 0.7 copy.41
  306.8 0.0 copy-done.5
  306.8 0.6 copy.42
  307.5 0.0 copy-done.1
  307.5 0.7 copy.43
  (3 shorter events, 0.0 us)
Async XLA Ops:
  0.6 8.6 %copy-start.3 = (bf16[768,96]{0,1:T(8,128)(2,1)S(1)}, bf16[768,96]{0,1:T(8,128)(2,1)}, u32[]{:S(2)}) copy-start(bf16[768,96]{0,1:T(8,128)(2,1)} %param.27) | copy-start | bytes 442372
  0.7 8.6 %copy-start.4 = (bf16[96,768]{1,0:T(8,128)(2,1)S(1)}, bf16[96,768]{1,0:T(8,128)(2,1)}, u32[]{:S(2)}) copy-start(bf16[96,768]{1,0:T(8,128)(2,1)} %param.25) | copy-start | bytes 442372
  302.2 2.8 copy-start
  304.9 1.2 copy-start.2
  304.9 1.9 copy-start.5
  304.9 2.5 copy-start.1

commit v4 on v3

--- a/solution.py
+++ b/solution.py
@@ -185,18 +185,18 @@
     def source_at(i):
         return sum(same(i, t, places) * source(t) for t in turns)
 
-    def vec_copy(i, sending):
-        di, zi = i // places, i % places
-        if sending:
-            slot = me * places + mz
-        else:
-            slot = ((me + count - di) % count) * places + (mz + places - zi) % places
+    def vec_z(s, sending):
+        to = (mz + s) % places
+        slot = mz if sending else (mz + places - s) % places
+        n = nbits + s
+        return remote(vec_ref, vb_ref.at[me, slot], vs.at[n], vr.at[n], (me, to))
+
+    def vec_d(b, sending):
+        size = 1 << b
+        holder = me if sending else flip(me, size)
+        held = pl.ds(holder // size * size, size)
         return remote(
-            vec_ref,
-            vb_ref.at[slot],
-            vs.at[i],
-            vr.at[i],
-            ((me + di) % count, (mz + zi) % places),
+            vb_ref.at[held], vb_ref.at[held], vs.at[b], vr.at[b], (flip(me, size), mz)
         )
 
     def z_copy(a, p, up, own=False):
@@ -287,18 +287,14 @@
     own = [
         pltpu.make_async_copy(w_ref.at[a], g_ref.at[a, mz, me], ls.at[a]) for a in range(3)
     ]
-    own_vec = pltpu.make_async_copy(vec_ref, vb_ref.at[me * places + mz], ls.at[3])
-
-    def send_vec(i, carry):
-        vec_copy(i, True).start()
-        return carry
-
-    lax.fori_loop(1, total, send_vec, 0)
+    own_vec = pltpu.make_async_copy(vec_ref, vb_ref.at[me, mz], ls.at[3])
+
+    for s in range(1, places):
+        vec_z(s, True).start()
     own_vec.start()
-    for j in [n for n, chunk in enumerate(chunks) if chunk[1] == 0]:
-        step(j, 0)
-    for a in range(3):
-        pass_on(a, mz, True)
+    own_steps = [n for n, chunk in enumerate(chunks) if chunk[1] == 0]
+    step(own_steps[0], 0)
+    pass_on(0, mz, True)
     for copy in own:
         copy.start()
 
@@ -306,14 +302,18 @@
     for i, table in enumerate(spread_turns(mine)):
         table_ref[i] = table
 
-    run(0, 2)
-
-    def wait_vec(i, carry):
-        vec_copy(i, False).wait_recv()
-        return carry
-
     own_vec.wait()
-    lax.fori_loop(1, total, wait_vec, 0)
+    for s in range(1, places):
+        vec_z(s, False).wait_recv()
+    for b in range(nbits):
+        vec_d(b, True).start()
+        if b == nbits - 1:
+            for j in own_steps[1:]:
+                step(j, 0)
+            run(0, 2)
+            for a in (1, 2):
+                pass_on(a, mz, True)
+        vec_d(b, False).wait_recv()
     values = vb_ref[...].reshape(total * 8, LANES)
     sub = lax.broadcasted_iota(jnp.int32, (total * 8, 1), 0)
     who, what = sub // 8, sub % 8
@@ -483,11 +483,10 @@
                 x_copy(h, p, True).wait_send()
 
 
-    def wait_sent(i, carry):
-        vec_copy(i, True).wait_send()
-        return carry
-
-    lax.fori_loop(1, total, wait_sent, 0)
+    for s in range(1, places):
+        vec_z(s, True).wait_send()
+    for b in range(nbits):
+        vec_d(b, True).wait_send()
     for a in range(3):
         for p in range(places):
 
@@ -508,7 +507,6 @@
 def front(block_input, cotangent, weights, vector, turns, count, places, wide, piece):
     rows, model = block_input.shape
     depth, ff = weights.shape[1:]
-    total = count * places
     heads = ff // GROUP
     sem = pltpu.SemaphoreType.DMA
     shape = jax.ShapeDtypeStruct
@@ -537,7 +535,7 @@
             pltpu.VMEM((model, rows), BF),
             pltpu.VMEM((model, rows), BF),
             pltpu.VMEM((3, rows, LANES), F32),
-            pltpu.VMEM((total, 8, LANES), F32),
+            pltpu.VMEM((count, places, 8, LANES), F32),
             pltpu.VMEM((places, ff), F32),
             pltpu.VMEM((places, ff), F32),
             pltpu.VMEM((places, model, ff), BF),
@@ -546,8 +544,8 @@
             sem((3 * places,)),
             sem((3 * places * (count - 1),)),
             sem((3 * places * (count - 1),)),
-            sem((total,)),
-            sem((total,)),
+            sem((count.bit_length() + places,)),
+            sem((count.bit_length() + places,)),
             sem((heads * places,)),
             sem((heads * places,)),
             sem((7 + heads + 2 * places,)),

time: 309 us -> 305 us (0.987)
    pallas_call x1, Pallas kernels: 126 us -> 121 us  [front(): pl.pallas_call(functools.partial(front_kernel, count, places, wide, piece...]
where the time goes in v4:
time: 305 us
  Pallas kernels  283 us (93%)
  local copies, waits for them, and re-layouts  16.4 us (5%)
  other arithmetic  4.69 us (2%)
    pallas_call x1, Pallas kernels, front(): pl.pallas_call(functools.partial(front_kernel, count, places, wide, piece...  121 us
    pallas_call x1, Pallas kernels, middle(): pl.pallas_call(functools.partial(middle_kernel, count, places, heads, wq,...  98.5 us
    pallas_call x1, Pallas kernels, tail(): pl.pallas_call(functools.partial(tail_kernel, count, places, wide, piece)...  63.6 us
    unnamed x19, local copies, waits for them, and re-layouts  8.94 us

profile of v4, /device:TPU:0, one launch (start us, length us, event | category | flops | bytes accessed | tf_op | source)
XLA Modules:
  0.0 304.6 jit_solution(16395837342417777705)
XLA Ops:
  0.6 0.0 copy-start.3
  0.7 0.0 copy-start.4
  0.7 0.7 pad_bitcast_fusion.4
  1.4 0.8 reshape.51
  2.1 0.7 bitcast_convert_fusion
  2.8 0.7 pad_bitcast_fusion.2
  3.5 0.7 pad_bitcast_fusion
  4.2 0.6 stack.63.vec_ref
  4.8 1.4 iota_subtract_fusion
  6.1 0.3 multiply_cosine_fusion
  6.5 0.7 pad_maximum_fusion.1.cs_ref.refs_2_
  7.1 1.1 copy.30
  8.2 0.8 maximum_bitcast_fusion
  9.1 0.1 copy.32
  9.2 0.0 copy-done.3
  9.2 0.0 copy-done.4
  9.2 0.8 pad_maximum_fusion.w_ref
  10.0 120.7 %front.1 = (bf16[3,4,512,256]{3,2,1,0:T(8,128)(2,1)}, bf16[4,8,96,768]{3,2,1,0:T(8,128)(2,1)}, f32[8,768]{1,0:T(8,128)}, f32[512,768]{1,0:T(8,128)}, f32[512,768...) custom-call(f32[512,768]{1,0:T(8,128)} %refs_0_.1, ...), custom_call_target="tpu_custom_call" | custom-call | tf_op jit(solution)/shard_map/front/pallas_call | solution.py:513
  130.7 98.5 %middle.1 = (bf16[4,3,512,256]{3,2,1,0:T(8,128)(2,1)}, f32[3,8,256]{2,1,0:T(8,128)}, bf16[2,4,96,768]{3,2,1,0:T(8,128)(2,1)}) custom-call(bf16[3,2048,256]{2,1,0:T(8,128)(2,1)} %bitcast.45, s32[1,2048]{1,0:T(1,128)} %bitcast.51, f32[16,2048]{1,0:T(8,128)} %pad_maximum_fusion.1.cs_ref.refs_2_, bf16[4,8,96,768]{3,2,1,0:T(8,128)(2,1)} %bitcast.43, ...), custom_call_target="tpu_custom_call" | custom-call | tf_op jit(solution)/shard_map/middle/pallas_call | solution.py:837
  229.2 63.6 %tail.1 = (f32[512,768]{1,0:T(8,128)}, f32[512,768]{1,0:T(8,128)}, f32[3,96,192]{2,1,0:T(8,128)}, f32[192,96]{1,0:T(8,128)}, f32[96,768]{1,0:T(8,128)}, /*index=5*/f32[768,96]{1,0:T(8,128)}, f32[8,128]{1,0:T(8,128)}) custom-call(f32[512,768]{1,0:T(8,128)} %refs_0_.1, f32[512,768]{1,0:T(8,128)} %refs_1_.1, ...), custom_call_target="tpu_custom_call" | custom-call | tf_op jit(solution)/shard_map/tail/pallas_call | solution.py:1122
  292.8 1.2 slice_bitcast_fusion.1
  294.0 0.7 slice_reduce_fusion
  294.7 1.4 slice_bitcast_fusion
  296.1 0.7 reshape_squeeze.3
  296.7 1.9 copy.33
  298.6 0.0 copy-start
  298.6 2.8 copy.39
  301.4 0.0 copy-done
  301.4 0.0 copy-start.2
  301.4 0.0 copy-start.5
  301.4 0.0 copy-start.1
  301.4 1.1 copy.40
  302.5 0.0 copy-done.2
  302.5 0.7 copy.41
  303.2 0.0 copy-done.5
  303.2 0.6 copy.42
  303.9 0.0 copy-done.1
  303.9 0.7 copy.43
  (3 shorter events, 0.0 us)
Async XLA Ops:
  0.6 8.6 %copy-start.3 = (bf16[768,96]{0,1:T(8,128)(2,1)S(1)}, bf16[768,96]{0,1:T(8,128)(2,1)}, u32[]{:S(2)}) copy-start(bf16[768,96]{0,1:T(8,128)(2,1)} %param.27) | copy-start | bytes 442372
  0.7 8.6 %copy-start.4 = (bf16[96,768]{1,0:T(8,128)(2,1)S(1)}, bf16[96,768]{1,0:T(8,128)(2,1)}, u32[]{:S(2)}) copy-start(bf16[96,768]{1,0:T(8,128)(2,1)} %param.25) | copy-start | bytes 442372
  298.6 2.8 copy-start
  301.4 1.2 copy-start.2
  301.4 1.9 copy-start.5
  301.4 2.5 copy-start.1
